TPU v7x, 512 devices: a whole 4x8x8 slice. The times are simulated.
512 devices in a mesh: orb: 32 (over x, y), grid: 16 (over z, core).
Axes of the slice: x: 4, y: 8, z: 8, core: 2. Of those that a mesh axis runs over, the one named last changes fastest.
Arguments:
- orbitals: float32 [128, 32, 4096], P('orb', 'grid'), may hold values from -6 to 6
- rotation: float32 [128, 128], replicated, may hold values from -0.5 to 0.5
- tile_list: int32 [64, 2], replicated, may hold values from 0 to 31, as said below
- pair_mask: int32 [128, 128], replicated, may hold values from 0 to 1, as said below
Outputs:
- exchange_term: float32 [128, 32, 4096], P('orb', 'grid')
Inputs may be any that keep to these rules, and one draw needn't show every extreme that they name: `tile_list`: row t names one tile: its target block and its source block of 4 orbitals each; no tile is named twice. `pair_mask`: among the 1024 orbital pairs that lie in listed tiles, exactly 512 are 1.
All inputs are finite; a program needn't handle non-finite values.
Results may differ from a plain program's by a relative error of at most 0.0003.
Values sent between devices are 32-bit elements; how exact they have to be, the bound alone decides.
A program may use at most 64 MiB of HBM per device.

v0:
```python
import jax
import jax.numpy as jnp
from jax import lax
from jax.sharding import PartitionSpec as P

NORB = 128
BLK = 4
NX = 32
NY = 64
NZ = 64
LIVE_DEV = 1


precise = lax.Precision.HIGHEST
coupling = 0.25
screening = 0.1


def split_up(array, dim, devices):
    dims = array.shape
    tiles = array.reshape(*dims[:dim], devices, dims[dim] // devices, *dims[dim + 1 :])
    return jnp.moveaxis(tiles, dim, 0)


def laid_out(tiles, dim):
    dims = list(tiles.shape[1:])
    dims[dim] *= tiles.shape[0]
    return jnp.moveaxis(tiles, 0, dim).reshape(dims)


def joined_exchange(array, axis, axes, splits, concats):
    sizes = [lax.axis_size(a) for a in axes]
    tiles = split_up(array, splits[0], sizes[0])
    tiles = jnp.moveaxis(split_up(tiles, splits[1] + 1, sizes[1]), 0, 1)
    inside = tiles.shape[2:]
    tiles = tiles.reshape(-1, *inside)
    tiles = lax.all_to_all(tiles, axis, split_axis=0, concat_axis=0, tiled=True)
    tiles = laid_out(tiles.reshape(*sizes, *inside), concats[0] + 1)
    return laid_out(tiles, concats[1])


def sine_table(length):
    wave_index = jnp.arange(length, dtype=jnp.float32) + 1.0
    return jnp.sqrt(2.0 / (length + 1.0)) * jnp.sin(
        jnp.pi * wave_index[:, None] * wave_index[None, :] / (length + 1.0)
    )


def eigen_values(length):
    wave_index = jnp.arange(length, dtype=jnp.float32) + 1.0
    return 2.0 - 2.0 * jnp.cos(jnp.pi * wave_index / (length + 1.0))


def green_kernel(size_x, size_y, size_z):
    summed = (
        eigen_values(size_x)[:, None, None]
        + eigen_values(size_y)[None, :, None]
        + eigen_values(size_z)[None, None, :]
    )
    return coupling / (summed + screening)


def pair_lists(tile_list, pair_mask):
    within = jnp.arange(BLK * BLK, dtype=jnp.int32)
    targets = (BLK * tile_list[:, 0:1] + within[None, :] // BLK).reshape(-1)
    sources = (BLK * tile_list[:, 1:2] + within[None, :] % BLK).reshape(-1)
    return (targets, sources, pair_mask[targets, sources])


def compact(targets, sources, live_flags, number):
    ranking = jnp.cumsum(live_flags) - 1
    places = jnp.where(live_flags == 1, ranking, number)
    picked = (
        jnp.zeros((number,), jnp.int32)
        .at[places]
        .set(jnp.arange(live_flags.shape[0], dtype=jnp.int32), mode="drop")
    )
    return (targets[picked], sources[picked])


def along_z(values, matrix):
    number, planes, width_yz = values.shape
    size_z = matrix.shape[0]
    shaped = values.reshape(number, planes, width_yz // size_z, size_z)
    return jnp.einsum("pxrz,zk->pxrk", shaped, matrix, precision=precise).reshape(
        number, planes, width_yz
    )


def along_y(values, matrix):
    number, planes, width_yz = values.shape
    size_y = matrix.shape[0]
    shaped = values.reshape(number, planes, size_y, width_yz // size_y)
    return jnp.einsum("pxyz,yk->pxkz", shaped, matrix, precision=precise).reshape(
        number, planes, width_yz
    )


def along_x(values, matrix):
    return jnp.einsum("pxc,xk->pkc", values, matrix, precision=precise)


def regroup(values, outer, middle):
    return values.reshape(outer, middle, -1).transpose(1, 0, 2).reshape(-1)


def on_device(orbitals, rotation, tile_list, pair_mask):
    rotated = jnp.einsum(
        "ij,ixc->jxc",
        rotation,
        lax.all_to_all(orbitals, "orb", split_axis=2, concat_axis=0, tiled=True),
        precision=precise,
    )
    planes = rotated.shape[1]
    width_yz = rotated.shape[2]
    targets, sources, live_flags = pair_lists(tile_list, pair_mask)
    weights = live_flags.astype(jnp.float32)
    matrix_x = sine_table(NX)
    matrix_y = sine_table(NY)
    matrix_z = sine_table(NZ)
    kernel = green_kernel(NX, NY, NZ).reshape(NX, NY * NZ)
    orbital_ids = jnp.arange(NORB, dtype=jnp.int32)
    targets, sources = compact(
        targets, sources, live_flags, LIVE_DEV * lax.axis_size("orb") * lax.axis_size("grid")
    )
    density = rotated[targets] * rotated[sources]
    number = density.shape[0]
    spectrum = along_z(density, matrix_z)
    spectrum = joined_exchange(spectrum, ("orb", "grid"), ("orb", "grid"), (0, 0), (2, 1))
    spectrum = along_x(along_y(spectrum, matrix_y), matrix_x) * kernel
    spectrum = along_y(along_x(spectrum, matrix_x), matrix_y)
    spectrum = joined_exchange(spectrum, ("orb", "grid"), ("orb", "grid"), (2, 1), (0, 0))
    outer = lax.axis_size("orb")
    middle = lax.axis_size("grid")
    targets = regroup(targets, outer, middle)
    sources = regroup(sources, outer, middle)
    weights = regroup(weights, outer, middle)
    potential = along_z(spectrum, matrix_z)
    products = potential * rotated[sources]
    selector = (targets[None, :] == orbital_ids[:, None]).astype(jnp.float32)
    partial_value = -jnp.dot(
        selector, products.reshape(number, planes * width_yz), precision=precise
    )
    partial_value = partial_value.reshape(NORB, planes, width_yz)
    return lax.all_to_all(partial_value, "orb", split_axis=0, concat_axis=2, tiled=True)


def solution(mesh):
    in_specs = (P("orb", "grid", None), P(), P(), P())
    out_specs = P("orb", "grid", None)
    return jax.shard_map(
        on_device, mesh=mesh, in_specs=in_specs, out_specs=out_specs, check_vma=False
    )
```

profile of v0, /device:TPU:1, one launch (start us, length us, event | category | flops | bytes accessed | tf_op | source)
XLA Modules:
  0.0 161.2 jit_solution(12426053909212209676)
XLA Ops:
  0.0 5.4 %copy.48 = f32[4,2,4096]{0,1,2:T(2,128)} copy(f32[4,2,4096]{2,1,0:T(2,128)} %param.4) | data formatting | bytes 262144 | tf_op args[0]
  5.4 8.6 %reshape.432 = f32[32,1,1024]{2,1,0:T(1,128)} reshape(f32[4096,2,4]{2,1,0:T(2,128)} %bitcast.97) | data formatting | bytes 262144
  14.0 10.5 %all-to-all-start = ((f32[32,1,1024]{2,1,0:T(1,128)}), f32[32,1,1024]{2,1,0:T(1,128)S(1)}, u32[]{:S(2)}, u32[]{:S(2)}) async-start(f32[32,1,1024]{2,1,0:T(1,128)} %reshape.432), calls=%async_computation | async-start | bytes 262144 | tf_op jit(solution)/shard_map/all_to_all | solution.py:111
  25.0 6.8 %gather_fusion = s32[1024]{0:T(1024)S(1)} fusion(s32[128,128]{1,0:T(8,128)S(1)} %copy-done.1, s32[1024]{0:T(1024)S(1)} %bitcast.95), kind=kCustom, calls=%fused_computation | custom fusion | bytes 16384 | tf_op jit(solution)/shard_map/gather | solution.py:67
  32.4 4.3 %scatter_custom_fusion = s32[512]{0:T(512)S(1)} fusion(s32[1024]{0:T(1024)S(1)} %bitcast.114, s32[1024]{0:T(1024)S(1)} %iota.52, s32[]{:T(128)} %constant.64.clone.1), kind=kCustom, calls=%fused_computation.80 | custom fusion | bytes 2052 | tf_op jit(solution)/shard_map/scatter | solution.py:76
  36.7 2.3 %gather_fusion.3 = s32[512]{0:T(512)S(1)} fusion(s32[1024]{0:T(1024)S(1)} %add.263, s32[1024]{0:T(1024)S(1)} %pad_clamp_fusion.3), kind=kCustom, calls=%fused_computation.3 | custom fusion | bytes 6144 | tf_op jit(solution)/shard_map/gather | solution.py:78
  39.0 2.3 %gather_fusion.1 = s32[512]{0:T(512)S(1)} fusion(s32[1024]{0:T(1024)S(1)} %add.248, s32[1024]{0:T(1024)S(1)} %pad_clamp_fusion.3), kind=kCustom, calls=%fused_computation.1 | custom fusion | bytes 6144 | tf_op jit(solution)/shard_map/gather | solution.py:78
  41.9 0.9 reduce.2
  42.9 7.8 %reshape.433 = f32[4096,2,4]{2,1,0:T(2,128)} reshape(f32[32,1024]{1,0:T(8,128)S(1)} %reduce.2) | data formatting | bytes 262144
  50.7 5.2 %copy.49 = f32[4,2,32,128]{3,0,2,1:T(4,128)S(1)} copy(f32[4,2,32,128]{0,1,3,2:T(2,128)} %bitcast.96) | data formatting | bytes 262144 | tf_op jit(solution)/shard_map/all_to_all | solution.py:111
  56.3 2.1 %gather_fusion.2 = f32[512,2,128]{2,1,0:T(2,128)S(1)} fusion(f32[128,2,128]{2,1,0:T(2,128)S(1)} %copy.51, s32[1024]{0:T(1024)S(1)} %pad_clamp_fusion.2), kind=kCustom, calls=%fused_computation.2 | custom fusion | bytes 1050624 | tf_op jit(solution)/shard_map/gather | solution.py:126
  58.3 2.1 %gather_fusion.4 = f32[512,2,128]{2,1,0:T(2,128)S(1)} fusion(f32[128,2,128]{2,1,0:T(2,128)S(1)} %copy.51, s32[1024]{0:T(1024)S(1)} %pad_clamp_fusion.1), kind=kCustom, calls=%fused_computation.4 | custom fusion | bytes 1050624 | tf_op jit(solution)/shard_map/gather | solution.py:126
  61.7 1.0 copy.54
  62.7 21.4 %all-to-all-start.1 = ((f32[512,1,2,128]{3,2,1,0:T(2,128)}), f32[512,1,2,128]{3,2,1,0:T(2,128)S(1)}, u32[]{:S(2)}, u32[]{:S(2)}) async-start(f32[512,1,2,128]{3,2,1,0:T(2,128)} %copy.54), calls=%async_computation.1 | async-start | bytes 1048576 | tf_op jit(solution)/shard_map/all_to_all | solution.py:37
  85.2 20.9 %all-to-all-done.1 = f32[512,1,2,128]{3,2,1,0:T(2,128)S(1)} async-done(((f32[512,1,2,128]{3,2,1,0:T(2,128)}), f32[512,1,2,128]{3,2,1,0:T(2,128)S(1)}, u32[]{:S(2)}, u32[]{:S(2)}) %all-to-all-start.1) | async-done | bytes 524320 | tf_op jit(solution)/shard_map/all_to_all | solution.py:37
  106.5 1.2 convolution_bitcast_fusion.1
  109.2 1.7 %fusion.4 = f32[32,64,64]{2,0,1:T(8,128)S(1)} fusion(f32[64,64,32]{1,0,2:T(8,128)S(1)} %dot_general.38, f32[32]{0:T(128)S(1)} %get-tuple-element.11, f32[32]{0:T(128)S(1)} %get-tuple-element.12), kind=kOutput, calls=%fused_computation.15 | convolution fusion | flops 50334720 | bytes 1048832 | tf_op jit(solution)/shard_map/pxc,xk->pkc/dot_general | solution.py:100
  110.9 1.8 %convolution_bitcast_fusion = f32[1,32,64,64]{3,2,1,0:T(8,128)S(1)} fusion(f32[32,64,64]{2,0,1:T(8,128)S(1)} %fusion.4, f32[64]{0:T(128)S(1)} %get-tuple-element.9, f32[64]{0:T(128)S(1)} %get-tuple-element.10), kind=kOutput, calls=%fused_computation.9 | convolution fusion | flops 100675584 | bytes 1049088 | tf_op jit(solution)/shard_map/pxyz,yk->pxkz/dot_general | solution.py:94
  112.8 1.1 copy.59
  113.9 8.9 %all-to-all-start.2 = ((f32[512,1,2,128]{3,2,1,0:T(2,128)}), f32[512,1,2,128]{3,2,1,0:T(2,128)S(1)}, u32[]{:S(2)}, u32[]{:S(2)}) async-start(f32[512,1,2,128]{3,2,1,0:T(2,128)} %bitcast.30), calls=%async_computation.2 | async-start | bytes 1048576 | tf_op jit(solution)/shard_map/all_to_all | solution.py:37
  123.3 2.1 %gather_fusion.5 = f32[512,2,128]{2,1,0:T(2,128)S(1)} fusion(f32[128,2,128]{2,1,0:T(2,128)S(1)} %copy.51, s32[1024]{0:T(1024)S(1)} %pad_clamp_fusion), kind=kCustom, calls=%fused_computation.5 | custom fusion | bytes 1050624 | tf_op jit(solution)/shard_map/gather | solution.py:139
  125.6 19.2 %all-to-all-done.2 = f32[512,1,2,128]{3,2,1,0:T(2,128)S(1)} async-done(((f32[512,1,2,128]{3,2,1,0:T(2,128)}), f32[512,1,2,128]{3,2,1,0:T(2,128)S(1)}, u32[]{:S(2)}, u32[]{:S(2)}) %all-to-all-start.2) | async-done | bytes 524320 | tf_op jit(solution)/shard_map/all_to_all | solution.py:37
  145.6 1.5 fusion.1
  147.7 12.8 %all_to_all.46 = f32[128,2,128]{2,1,0:T(2,128)S(1)} all-to-all(f32[128,2,128]{2,1,0:T(2,128)S(1)} %reshape.368), channel_id=1, replica_groups=mesh['orb'=32,'grid'=16] {'orb'}, dimensions={0} | all-to-all | bytes 262144 | tf_op jit(solution)/shard_map/all_to_all | solution.py:145
  (69 shorter events, 9.2 us)
Async XLA Ops:
  0.0 55.8 %copy-start = (f32[128,128]{1,0:T(8,128)S(1)}, f32[128,128]{1,0:T(8,128)}, u32[]{:S(2)}) copy-start(f32[128,128]{1,0:T(8,128)} %param.5) | copy-start | bytes 196612
  0.0 24.5 %copy-start.2 = (s32[64,2]{0,1:T(2,128)S(1)}, s32[64,2]{0,1:T(2,128)}, u32[]{:S(2)}) copy-start(s32[64,2]{0,1:T(2,128)} %param.6) | copy-start | bytes 1540
  0.0 24.9 %copy-start.1 = (s32[128,128]{1,0:T(8,128)S(1)}, s32[128,128]{1,0:T(8,128)}, u32[]{:S(2)}) copy-start(s32[128,128]{1,0:T(8,128)} %param.7) | copy-start | bytes 196612
  14.0 27.4 %all-to-all-start = ((f32[32,1,1024]{2,1,0:T(1,128)}), f32[32,1,1024]{2,1,0:T(1,128)S(1)}, u32[]{:S(2)}, u32[]{:S(2)}) async-start(f32[32,1,1024]{2,1,0:T(1,128)} %reshape.432), calls=%async_computation | async-start | bytes 262144 | tf_op jit(solution)/shard_map/all_to_all | solution.py:111
  62.7 43.3 %all-to-all-start.1 = ((f32[512,1,2,128]{3,2,1,0:T(2,128)}), f32[512,1,2,128]{3,2,1,0:T(2,128)S(1)}, u32[]{:S(2)}, u32[]{:S(2)}) async-start(f32[512,1,2,128]{3,2,1,0:T(2,128)} %copy.54), calls=%async_computation.1 | async-start | bytes 1048576 | tf_op jit(solution)/shard_map/all_to_all | solution.py:37
  113.9 30.9 %all-to-all-start.2 = ((f32[512,1,2,128]{3,2,1,0:T(2,128)}), f32[512,1,2,128]{3,2,1,0:T(2,128)S(1)}, u32[]{:S(2)}, u32[]{:S(2)}) async-start(f32[512,1,2,128]{3,2,1,0:T(2,128)} %bitcast.30), calls=%async_computation.2 | async-start | bytes 1048576 | tf_op jit(solution)/shard_map/all_to_all | solution.py:37
where the time goes:
time: 162 us; the launch traced here: 161 us
  local copies, waits for them, and re-layouts  56.7 us (35%)
  starting transfers between devices  40.8 us (25%)
  waiting for transfers between devices  40.1 us (25%)
  blocking collectives  12.8 us (8%)
  matrix products  8.42 us (5%)
  other arithmetic  2.05 us (1%)
    all_to_all x2, waiting for transfers between devices, joined_exchange(): tiles = lax.all_to_all(tiles, axis, split_axis=0, concat_axis=0, tiled=True)  40.1 us
    all_to_all x2, starting transfers between devices, joined_exchange(): tiles = lax.all_to_all(tiles, axis, split_axis=0, concat_axis=0, tiled=True)  30.3 us
    unnamed x9, local copies, waits for them, and re-layouts  21.8 us
    all_to_all x1, blocking collectives, on_device(): lax.all_to_all(partial_value, 'orb', split_axis=0, concat_axis=2, tiled=T...  12.8 us
    all_to_all x1, starting transfers between devices, on_device(): lax.all_to_all(orbitals, 'orb', split_axis=2, concat_axis=0, tiled=True)  10.5 us
    gather x1, local copies, waits for them, and re-layouts, pair_lists(): return (targets, sources, pair_mask[targets, sources])  6.8 us
    all_to_all x2, local copies, waits for them, and re-layouts, on_device(): lax.all_to_all(orbitals, 'orb', split_axis=2, concat_axis=0, tiled=True)  5.67 us
    gather x2, local copies, waits for them, and re-layouts, compact(): return (targets[picked], sources[picked])  4.58 us
  transfers between devices with their start and end apart: 3, of which 2 were waited for; matrix products, arithmetic and copies ran while one was open for 13% of the time, Pallas kernels for 0%

commit v1 on v0

v1 whole, which is shorter than its diff:
```python
import numpy as np
import jax
import jax.numpy as jnp
from jax import lax
from jax.experimental import pallas as pl
from jax.experimental.pallas import tpu as pltpu
from jax.sharding import PartitionSpec as P

NORB = 128
NX = 32
NY = 64
NZ = 64
NPAIR = 1024
LANES = 128
N_ORB = 32
N_GRID = 16
XDIM = 4
YDIM = 8
ZDIM = 8
ROWS = 1024
PREP = 256
coupling = 0.25
screening = 0.1
MESH = pl.DeviceIdType.MESH
f32 = jnp.float32
bf16 = jnp.bfloat16


def sine_table(length):
    k = np.arange(length, dtype=np.float64) + 1.0
    return np.sqrt(2.0 / (length + 1.0)) * np.sin(np.pi * k[:, None] * k[None, :] / (length + 1.0))


def eigen_values(length):
    k = np.arange(length, dtype=np.float64) + 1.0
    return 2.0 - 2.0 * np.cos(np.pi * k / (length + 1.0))


def halves(table):
    high = table.astype(np.float32).astype(jnp.bfloat16)
    low = (table - high.astype(np.float64)).astype(np.float32).astype(jnp.bfloat16)
    return high, low


def tables():
    sx_h, sx_l = halves(sine_table(NX))
    table_x = np.concatenate([sx_h, sx_h, sx_l], axis=1)
    s = sine_table(NY)
    split_cols = np.concatenate([s[:, 0::2], s[:, 1::2]], axis=1)
    fh, fl = halves(split_cols)
    table_yf = np.concatenate([fh, fh, fl], axis=1)
    ih, il = halves(split_cols.T)
    table_yi = np.concatenate([ih, ih, il], axis=1)
    block = np.kron(np.eye(2), sine_table(NZ))
    bh, bl = halves(block)
    table_z = np.concatenate([bh, bl], axis=1)
    ly, lz, lx = eigen_values(NY), eigen_values(NZ), eigen_values(NX)
    sum_yz = ly[:, None] + np.tile(lz, 2)[None, :] + screening
    sum_x = np.repeat(lx.reshape(NX // 2, 2), NZ, axis=1)
    return (
        table_x,
        table_yf,
        table_yi,
        table_z,
        sum_yz.astype(np.float32),
        sum_x.astype(np.float32),
    )


def split(v):
    high = v.astype(bf16)
    low = (v - high.astype(f32)).astype(bf16)
    return high, low


def dot(a, b):
    return jnp.dot(a, b, preferred_element_type=f32)


def dot_nt(a, b):
    return lax.dot_general(a, b, (((1,), (1,)), ((), ())), preferred_element_type=f32)


def iota(shape, dim):
    return lax.broadcasted_iota(jnp.int32, shape, dim)


def one_hot(cond):
    return jnp.where(cond, 1.0, 0.0).astype(bf16)


def z_product(v, table_z):
    high, low = split(v)
    a = dot(high, table_z)
    return a[:, :LANES] + a[:, LANES:] + dot(low, table_z[:, :LANES])


def kernel(
    orb_ref, rotation_ref, tile_ref, mask_ref, tx_ref, tyf_ref, tyi_ref, tz_ref, syz_ref, sx_ref,
    out_ref,
    own, got, sel_i, sel_j, sel_t, rot_k, rot_j, green, dens,
    ra, rb, box, mid, pot, ra2, rb2, back, term, gathered,
    in_sem, out_sem,
    e1_s, e1_r, a1_s, a1_r, b1_s, b1_r, a2_s, b2_s, x_ra, x_rb,
    c1_s, c1_r, d1_s, d1_r, c2_s, c2_r, d2_s, d2_r, e4_s, e4_r,
):
    o = lax.axis_index("orb")
    g = lax.axis_index("grid")
    x, y = o // YDIM, o % YDIM
    z, c = g // 2, g % 2

    def orb_peer(d):
        return ((x + d // YDIM) % XDIM) * YDIM + (y + d % YDIM) % YDIM

    def to_orb(src, dst, s_sem, r_sem, o2):
        return pltpu.make_async_remote_copy(
            src_ref=src, dst_ref=dst, send_sem=s_sem, recv_sem=r_sem,
            device_id=(o2, g), device_id_type=MESH,
        )

    def to_grid(src, dst, s_sem, r_sem, g2):
        return pltpu.make_async_remote_copy(
            src_ref=src, dst_ref=dst, send_sem=s_sem, recv_sem=r_sem,
            device_id=(o, g2), device_id_type=MESH,
        )

    def arrived(ref, sem):
        pltpu.make_async_copy(ref, ref, sem).wait()

    def orb_order(d):
        return (d * 11) % N_ORB

    def z_order(d):
        return (z + (d * 3) % ZDIM) % ZDIM

    for k in range(4):
        pltpu.make_async_copy(orb_ref.at[k], own.at[pl.ds(2 * k, 2), :], in_sem.at[k]).start()
    barrier = pltpu.get_barrier_semaphore()

    @pl.loop(1, N_ORB)
    def _(d):
        pl.semaphore_signal(barrier, inc=1, device_id=(orb_peer(d), g), device_id_type=MESH)

    @pl.loop(1, N_GRID)
    def _(d):
        g2 = ((z + d // 2) % ZDIM) * 2 + (c + d) % 2
        pl.semaphore_signal(barrier, inc=1, device_id=(o, g2), device_id_type=MESH)

    for k in range(4):
        pltpu.make_async_copy(orb_ref.at[k], own.at[pl.ds(2 * k, 2), :], in_sem.at[k]).wait()
    pl.semaphore_wait(barrier, N_ORB - 1 + N_GRID - 1)

    def cells(o2):
        return pl.ds(pl.multiple_of(o2 * LANES, LANES), LANES)

    pltpu.make_async_copy(own.at[:, cells(o)], got.at[o], e1_r).start()

    @pl.loop(1, N_ORB)
    def _(d):
        o2 = orb_peer(orb_order(d))
        to_orb(own.at[:, cells(o2)], got.at[o], e1_s, e1_r, o2).start()

    tiles = tile_ref[...].astype(f32)
    p_lane = iota((64, NPAIR), 1)
    in_tile = p_lane // 16 == iota((64, NPAIR), 0)
    p_row = iota((1, NPAIR), 1)
    target = 4.0 * jnp.sum(jnp.where(in_tile, tiles[:, 0:1], 0.0), axis=0, keepdims=True)
    target = target + (p_row // 4 % 4).astype(f32)
    source = 4.0 * jnp.sum(jnp.where(in_tile, tiles[:, 1:2], 0.0), axis=0, keepdims=True)
    source = source + (p_row % 4).astype(f32)
    half = (iota((256, NPAIR), 0) // 2).astype(f32)
    hot_i = one_hot(half == target)
    hot_j = one_hot(half == source)
    orb_row = iota((NORB, NPAIR), 0).astype(f32)
    mask_of = dot(mask_ref[...].astype(f32).astype(bf16), one_hot(orb_row == source))
    live = jnp.sum(jnp.where(orb_row == target, mask_of, 0.0), axis=0, keepdims=True)
    before = one_hot(iota((LANES, LANES), 0) < iota((LANES, LANES), 1))
    every = jnp.ones((LANES, LANES), bf16)
    running = jnp.zeros((8, LANES), f32)
    ranks = []
    for k in range(NPAIR // LANES):
        flags = jnp.broadcast_to(live[:, k * LANES : (k + 1) * LANES], (8, LANES))
        bits = flags.astype(bf16)
        rank = dot(bits, before) + running
        running = running + dot(bits, every)
        ranks.append(jnp.where(flags > 0.5, rank, -1.0)[0:1, :])
    rank = jnp.concatenate(ranks, axis=1)

    same_plane = iota((PREP, 256), 0) % 2 == iota((PREP, 256), 1) % 2

    def select_rows(r, carry):
        rows = pl.ds(pl.multiple_of(r * PREP, PREP), PREP)
        slot = ((iota((PREP, NPAIR), 0) + r * PREP) // 2).astype(f32)
        chosen = one_hot(slot == rank)
        sel_i[rows, :] = jnp.where(same_plane, dot_nt(chosen, hot_i), 0.0).astype(bf16)
        sel_j[rows, :] = jnp.where(same_plane, dot_nt(chosen, hot_j), 0.0).astype(bf16)
        sel_t[r] = jnp.where(same_plane, dot_nt(hot_i, chosen), 0.0).astype(bf16)
        return carry

    lax.fori_loop(0, ROWS // PREP, select_rows, 0)

    widen = one_hot(iota((256, NORB), 0) // 2 == iota((256, NORB), 1))
    widen_t = one_hot(iota((NORB, 256), 0) == iota((NORB, 256), 1) // 2)
    for k, part in enumerate(split(rotation_ref[...])):
        tall = dot_nt(widen, part).astype(bf16)
        rot_k[k] = jnp.where(same_plane, dot(tall, widen_t), 0.0).astype(bf16)

    def fill_green(k, carry):
        green[k] = coupling / (syz_ref[...] + sx_ref[pl.ds(k, 1), :])
        return carry

    lax.fori_loop(0, NX // 2, fill_green, 0)

    arrived(got, e1_r)

    got_h, got_l = split(got[...].reshape(256, LANES))
    rotated = dot(rot_k[0], got_h) + dot(rot_k[0], got_l) + dot(rot_k[1], got_h)
    rotated = jnp.concatenate(split(rotated), axis=1)

    def density_rows(r, carry):
        rows = pl.ds(pl.multiple_of(r * 128, 128), 128)
        wide_i = dot(sel_i[rows, :], rotated)
        wide_j = dot(sel_j[rows, :], rotated)
        at_j = wide_j[:, :LANES] + wide_j[:, LANES:]
        rot_j[rows, :] = at_j
        density = (wide_i[:, :LANES] + wide_i[:, LANES:]) * at_j
        spectrum = z_product(density, tz_ref[...])
        dens[pl.ds(r * 4, 4)] = spectrum.reshape(4, 32, LANES)
        return carry

    lax.fori_loop(0, ROWS // 128, density_rows, 0)

    ours = pl.ds(2 * g, 2)

    def z_rows(z2):
        return pl.ds(2 * z2, 2)

    def z_rows_b(z2):
        return pl.ds(16 + 2 * z2, 2)

    pltpu.make_async_copy(dens.at[o, pl.ds(0, 16), :], ra.at[o], a1_r).start()

    @pl.loop(1, N_ORB)
    def _(d):
        o2 = orb_peer(orb_order(d))
        to_orb(dens.at[o2, pl.ds(0, 16), :], ra.at[o], a1_s, a1_r, o2).start()

    @pl.when(c == 1)
    def _():
        pltpu.make_async_copy(dens.at[:, z_rows_b(z), :], rb.at[:, ours, :], b1_r).start()

    @pl.when(c == 0)
    def _():
        to_grid(dens.at[:, z_rows_b(z), :], rb.at[:, ours, :], b1_s, b1_r, 2 * z + 1).start()

    @pl.loop(1, ZDIM)
    def _(d):
        z2 = z_order(d)
        to_grid(dens.at[:, z_rows_b(z2), :], rb.at[:, ours, :], b1_s, b1_r, 2 * z2 + 1).start()

    arrived(ra, a1_r)

    @pl.when(c == 0)
    def _():
        pltpu.make_async_copy(ra.at[:, z_rows(z), :], box.at[:, ours, :], x_ra).start()

    @pl.when(c == 1)
    def _():
        to_grid(ra.at[:, z_rows(z), :], box.at[:, ours, :], a2_s, x_ra, 2 * z).start()

    @pl.loop(1, ZDIM)
    def _(d):
        z2 = z_order(d)
        to_grid(ra.at[:, z_rows(z2), :], box.at[:, ours, :], a2_s, x_ra, 2 * z2).start()

    @pl.when(c == 1)
    def _():
        arrived(rb, b1_r)
        pltpu.make_async_copy(rb.at[o], box.at[o], x_rb).start()

        @pl.loop(1, N_ORB)
        def _(d):
            o2 = orb_peer(orb_order(d))
            to_orb(rb.at[o2], box.at[o], b2_s, x_rb, o2).start()

        arrived(box, x_rb)

    @pl.when(c == 0)
    def _():
        arrived(box, x_ra)

    def along_x(src, dst):
        def step(r, carry):
            v = src[pl.ds(r * 4, 4)]
            v = jnp.concatenate([v[k] for k in range(4)], axis=1)
            high, low = split(v)
            w = dot(tx_ref[...], jnp.concatenate([high, low, high], axis=0))
            for k in range(4):
                dst[pl.ds(pl.multiple_of((r * 4 + k) * NX, NX), NX), :] = w[:, k * LANES : (k + 1) * LANES]
            return carry

        lax.fori_loop(0, N_ORB // 4, step, 0)

    along_x(box, mid)
    low_half = iota((N_ORB, LANES), 1) < NZ

    for k in range(NX // 2):
        v0 = mid[pl.ds(2 * k, N_ORB, stride=NX), :]
        v1 = mid[pl.ds(2 * k + 1, N_ORB, stride=NX), :]
        even = jnp.where(low_half, v0, pltpu.roll(v1, NZ, 1))
        odd = jnp.where(low_half, pltpu.roll(v0, NZ, 1), v1)
        high, low = split(jnp.concatenate([even, odd], axis=0))
        spectrum = dot(tyf_ref[...], jnp.concatenate([high, low, high], axis=0)) * green[k]
        high, low = split(spectrum)
        w = dot(tyi_ref[...], jnp.concatenate([high, low, high], axis=0))
        even, odd = w[:N_ORB], w[N_ORB:]
        mid[pl.ds(2 * k, N_ORB, stride=NX), :] = jnp.where(low_half, even, pltpu.roll(odd, NZ, 1))
        mid[pl.ds(2 * k + 1, N_ORB, stride=NX), :] = jnp.where(low_half, pltpu.roll(even, NZ, 1), odd)

    def back_x(r, carry):
        v = jnp.concatenate(
            [mid[pl.ds(pl.multiple_of((r * 4 + k) * NX, NX), NX), :] for k in range(4)], axis=1
        )
        high, low = split(v)
        w = dot(tx_ref[...], jnp.concatenate([high, low, high], axis=0))
        for k in range(4):
            pot[r * 4 + k] = w[:, k * LANES : (k + 1) * LANES]
        return carry

    lax.fori_loop(0, N_ORB // 4, back_x, 0)

    @pl.when(c == 0)
    def _():
        pltpu.make_async_copy(pot.at[:, ours, :], ra2.at[:, z_rows(z), :], c1_r).start()

        @pl.loop(1, N_GRID)
        def _(d):
            g2 = ((z + (d // 2) * 3) % ZDIM) * 2 + (c + d) % 2
            to_grid(pot.at[:, pl.ds(2 * g2, 2), :], ra2.at[:, z_rows(z), :], c1_s, c1_r, g2).start()

    @pl.when(c == 1)
    def _():
        pltpu.make_async_copy(pot.at[o], rb2.at[o], d1_r).start()

        @pl.loop(1, N_ORB)
        def _(d):
            o2 = orb_peer(orb_order(d))
            to_orb(pot.at[o2], rb2.at[o], d1_s, d1_r, o2).start()

    arrived(ra2, c1_r)
    pltpu.make_async_copy(ra2.at[o], back.at[o, pl.ds(0, 16), :], c2_r).start()

    @pl.loop(1, N_ORB)
    def _(d):
        o2 = orb_peer(orb_order(d))
        to_orb(ra2.at[o2], back.at[o, pl.ds(0, 16), :], c2_s, c2_r, o2).start()

    @pl.when(c == 1)
    def _():
        arrived(rb2, d1_r)
        pltpu.make_async_copy(rb2.at[:, ours, :], back.at[:, z_rows_b(z), :], d2_r).start()

        @pl.loop(1, N_GRID)
        def _(d):
            g2 = ((z + (d // 2) * 3) % ZDIM) * 2 + (c + d) % 2
            to_grid(rb2.at[:, pl.ds(2 * g2, 2), :], back.at[:, z_rows_b(z), :], d2_s, d2_r, g2).start()

    arrived(back.at[:, pl.ds(0, 16), :], c2_r)
    arrived(back.at[:, pl.ds(16, 16), :], d2_r)

    total = jnp.zeros((256, 2 * LANES), f32)
    for r in range(ROWS // PREP):
        rows = pl.ds(r * PREP, PREP)
        potential = z_product(back[pl.ds(r * 8, 8)].reshape(PREP, LANES), tz_ref[...])
        products = jnp.concatenate(split(potential * rot_j[rows, :]), axis=1)
        total = total + dot(sel_t[r], products)
    term[...] = (-(total[:, :LANES] + total[:, LANES:])).reshape(N_ORB, 8, LANES)

    pltpu.make_async_copy(term.at[o], gathered.at[:, cells(o)], e4_r).start()

    @pl.loop(1, N_ORB)
    def _(d):
        o2 = orb_peer(orb_order(d))
        to_orb(term.at[o2], gathered.at[:, cells(o)], e4_s, e4_r, o2).start()

    most = pl.ds(0, N_ORB - 1)
    arrived(got.at[most], e1_s)
    arrived(ra.at[most], a1_s)
    arrived(term.at[most], e4_s)
    arrived(ra2.at[most], c2_s)

    @pl.when(c == 0)
    def _():
        arrived(rb.at[:, pl.ds(0, 16), :], b1_s)
        arrived(ra.at[:, pl.ds(0, 14), :], a2_s)
        arrived(pot.at[:, pl.ds(0, 30), :], c1_s)

    @pl.when(c == 1)
    def _():
        arrived(rb.at[:, pl.ds(0, 14), :], b1_s)
        arrived(ra.at[:, pl.ds(0, 16), :], a2_s)
        arrived(rb.at[most], b2_s)
        arrived(pot.at[most], d1_s)
        arrived(rb2.at[:, pl.ds(0, 30), :], d2_s)

    arrived(gathered, e4_r)
    for k in range(4):
        pltpu.make_async_copy(gathered.at[pl.ds(2 * k, 2), :], out_ref.at[k], out_sem.at[k]).start()
    for k in range(4):
        pltpu.make_async_copy(gathered.at[pl.ds(2 * k, 2), :], out_ref.at[k], out_sem.at[k]).wait()


def on_device(orbitals, rotation, tile_list, pair_mask):
    consts = [jnp.asarray(t) for t in tables()]
    vmem = pl.BlockSpec(memory_space=pltpu.VMEM)
    anyspace = pl.BlockSpec(memory_space=pl.ANY)
    dma = pltpu.SemaphoreType.DMA
    box = pltpu.VMEM((N_ORB, NX, LANES), f32)
    half_box = pltpu.VMEM((N_ORB, 16, LANES), f32)
    return pl.pallas_call(
        kernel,
        out_shape=jax.ShapeDtypeStruct(orbitals.shape, f32),
        in_specs=[anyspace] + [vmem] * (3 + len(consts)),
        out_specs=anyspace,
        scratch_shapes=[
            pltpu.VMEM((8, NY * NZ), f32),
            pltpu.VMEM((N_ORB, 8, LANES), f32),
            pltpu.VMEM((ROWS, 256), bf16),
            pltpu.VMEM((ROWS, 256), bf16),
            pltpu.VMEM((ROWS // PREP, 256, PREP), bf16),
            pltpu.VMEM((2, 256, 256), bf16),
            pltpu.VMEM((ROWS, LANES), f32),
            pltpu.VMEM((NX // 2, NY, LANES), f32),
            box,
            half_box,
            box,
            box,
            pltpu.VMEM((N_ORB * NX, LANES), f32),
            box,
            half_box,
            box,
            box,
            pltpu.VMEM((N_ORB, 8, LANES), f32),
            pltpu.VMEM((8, NY * NZ), f32),
            dma((4,)),
            dma((4,)),
        ]
        + [dma] * 20,
        compiler_params=pltpu.CompilerParams(
            collective_id=0, has_side_effects=True, vmem_limit_bytes=48 * 2**20
        ),
    )(orbitals, rotation, tile_list, pair_mask, *consts)


def solution(mesh):
    in_specs = (P("orb", "grid", None), P(), P(), P())
    out_specs = P("orb", "grid", None)
    return jax.shard_map(
        on_device, mesh=mesh, in_specs=in_specs, out_specs=out_specs, check_vma=False
    )
```

time: 162 us -> 81 us (0.50)
  Pallas kernels: 0 us -> 73.3 us
  local copies, waits for them, and re-layouts: 56.7 us -> 7.07 us
  starting transfers between devices: 40.8 us -> 0 us
  waiting for transfers between devices: 40.1 us -> 0 us
  blocking collectives: 12.8 us -> 0 us
  matrix products: 8.42 us -> 0 us
  other arithmetic: 2.05 us -> 0 us
    pallas_call x0 -> x1, Pallas kernels: none -> 73.3 us  [on_device(): pl.pallas_call(kernel, out_shape=jax.ShapeDtypeStruct(orbitals.shape, f32...]
    all_to_all x3 -> x0, starting transfers between devices: 40.8 us -> none  [the longest x2 30.3 us: joined_exchange(): tiles = lax.all_to_all(tiles, axis, split_axis=0, concat_axis=0, tiled=True)]
    all_to_all x3 -> x0, waiting for transfers between devices: 40.1 us -> none  [the longest x2 40.1 us: joined_exchange(): tiles = lax.all_to_all(tiles, axis, split_axis=0, concat_axis=0, tiled=True)]
    gather x7 -> x0, local copies, waits for them, and re-layouts: 17.8 us -> none  [the longest x1 6.8 us: pair_lists(): return (targets, sources, pair_mask[targets, sources])]
    unnamed x9 -> x20, local copies, waits for them, and re-layouts: 21.8 us -> 7.07 us
    all_to_all x1 -> x0, blocking collectives: 12.8 us -> none  [on_device(): lax.all_to_all(partial_value, 'orb', split_axis=0, concat_axis=2, tiled=T...]
    dot_general x8 -> x0, matrix products: 8.42 us -> none  [the longest x2 2.97 us: along_y(): jnp.einsum('pxyz,yk->pxkz', shaped, matrix, precision=precise)]
    all_to_all x6 -> x0, local copies, waits for them, and re-layouts: 6.49 us -> none  [the longest x2 5.67 us: on_device(): lax.all_to_all(orbitals, 'orb', split_axis=2, concat_axis=0, tiled=True)]
  transfers between devices with their start and end apart: 3 -> 0, of which waited for: 2 -> 0; matrix products, arithmetic and copies ran while one was open for 13% -> 0% of each run, Pallas kernels for 0% -> 0%
where the time goes in v1:
time: 81 us; the launch traced here: 80.4 us
  Pallas kernels  73.3 us (90%)
  local copies, waits for them, and re-layouts  7.07 us (9%)
    pallas_call x1, Pallas kernels, on_device(): pl.pallas_call(kernel, out_shape=jax.ShapeDtypeStruct(orbitals.shape, f32...  73.3 us
    unnamed x20, local copies, waits for them, and re-layouts  7.07 us

profile of v1, /device:TPU:1, one launch (start us, length us, event | category | flops | bytes accessed | tf_op | source)
XLA Modules:
  0.0 80.4 jit_solution(16468938788775628005)
XLA Ops:
  0.0 0.0 copy-start.4
  0.0 0.0 copy-start.7
  0.0 0.8 copy.11.tile_ref
  0.8 0.0 copy-done.4
  0.8 0.0 copy-done.7
  0.8 0.0 copy-start
  0.8 0.9 %copy-done = f32[4,2,4096]{2,1,0:T(2,128)S(1)} copy-done((f32[4,2,4096]{2,1,0:T(2,128)S(1)}, f32[4,2,4096]{2,1,0:T(2,128)}, u32[]{:S(2)}) %copy-start) | copy-done | bytes 131096
  1.7 0.0 copy-start.1
  1.7 0.8 %copy-done.1 = f32[128,128]{1,0:T(8,128)S(1)} copy-done((f32[128,128]{1,0:T(8,128)S(1)}, f32[128,128]{1,0:T(8,128)}, u32[]{:S(2)}) %copy-start.1) | copy-done | bytes 65560
  2.5 0.0 copy-start.2
  2.5 0.8 %copy-done.2 = s32[128,128]{1,0:T(8,128)S(1)} copy-done((s32[128,128]{1,0:T(8,128)S(1)}, s32[128,128]{1,0:T(8,128)}, u32[]{:S(2)}) %copy-start.2) | copy-done | bytes 65560
  3.4 0.0 copy-start.3
  3.4 0.8 %copy-done.3 = bf16[128,256]{1,0:T(8,128)(2,1)S(1)} copy-done((bf16[128,256]{1,0:T(8,128)(2,1)S(1)}, bf16[128,256]{1,0:T(8,128)(2,1)}, u32[]{:S(2)}) %copy-start.3) | copy-done | bytes 65560
  4.2 0.0 copy-start.5
  4.2 0.8 copy-done.5
  5.0 0.0 copy-start.6
  5.0 0.8 copy-done.6
  5.7 0.0 copy-start.8
  5.7 0.7 copy-done.8
  6.4 73.3 %shard_map.100 = f32[4,2,4096]{2,1,0:T(2,128)S(1)} custom-call(f32[4,2,4096]{2,1,0:T(2,128)S(1)} %copy-done, f32[128,128]{1,0:T(8,128)S(1)} %copy-done.1, s32[64,2]{1,0:T(8,128)S(1)} %copy.11.tile_ref, s32[128,128]{1,0:T(8,128)S(1)} %copy-done.2, bf16[32,96]{1,0:T(8,128)(2,1)S(1)} %copy-done.8, bf16[64,192]{1,0:T(8,128)(2,1)S(1)} %copy-done.6, ...), custom_call_target="tpu_custom_call" | custom-call | tf_op jit(solution)/shard_map/pallas_call | solution.py:420
  79.8 0.7 copy.13
Async XLA Ops:
  0.0 0.8 copy-start.4
  0.0 0.8 copy-start.7
  0.8 0.9 %copy-start = (f32[4,2,4096]{2,1,0:T(2,128)S(1)}, f32[4,2,4096]{2,1,0:T(2,128)}, u32[]{:S(2)}) copy-start(f32[4,2,4096]{2,1,0:T(2,128)} %orb_ref.1) | copy-start | bytes 393220
  1.7 0.8 %copy-start.1 = (f32[128,128]{1,0:T(8,128)S(1)}, f32[128,128]{1,0:T(8,128)}, u32[]{:S(2)}) copy-start(f32[128,128]{1,0:T(8,128)} %rotation_ref.1) | copy-start | bytes 196612
  2.5 0.8 %copy-start.2 = (s32[128,128]{1,0:T(8,128)S(1)}, s32[128,128]{1,0:T(8,128)}, u32[]{:S(2)}) copy-start(s32[128,128]{1,0:T(8,128)} %mask_ref.1) | copy-start | bytes 196612
  3.4 0.8 %copy-start.3 = (bf16[128,256]{1,0:T(8,128)(2,1)S(1)}, bf16[128,256]{1,0:T(8,128)(2,1)}, u32[]{:S(2)}) copy-start(bf16[128,256]{1,0:T(8,128)(2,1)} %constant.15.clone.tz_ref) | copy-start | bytes 196612
  4.2 0.8 copy-start.5
  5.0 0.8 copy-start.6
  5.7 0.7 copy-start.8

commit v2 on v1

v2 whole, which is shorter than its diff:
```python
import numpy as np
import jax
import jax.numpy as jnp
from jax import lax
from jax.experimental import pallas as pl
from jax.experimental.pallas import tpu as pltpu
from jax.sharding import PartitionSpec as P

NORB = 128
NX = 32
NY = 64
NZ = 64
NPAIR = 1024
LANES = 128
N_ORB = 32
N_GRID = 16
XDIM = 4
YDIM = 8
ZDIM = 8
DX = (2, 1, 3, 0)
ROWS = 1024
PREP = 256
coupling = 0.25
screening = 0.1
MESH = pl.DeviceIdType.MESH
f32 = jnp.float32
bf16 = jnp.bfloat16


def sine_table(length):
    k = np.arange(length, dtype=np.float64) + 1.0
    return np.sqrt(2.0 / (length + 1.0)) * np.sin(np.pi * k[:, None] * k[None, :] / (length + 1.0))


def eigen_values(length):
    k = np.arange(length, dtype=np.float64) + 1.0
    return 2.0 - 2.0 * np.cos(np.pi * k / (length + 1.0))


def halves(table):
    high = table.astype(np.float32).astype(jnp.bfloat16)
    low = (table - high.astype(np.float64)).astype(np.float32).astype(jnp.bfloat16)
    return high, low


def tables():
    sx_h, sx_l = halves(sine_table(NX))
    table_x = np.concatenate([sx_h, sx_h, sx_l], axis=1)
    s = sine_table(NY)
    split_cols = np.concatenate([s[:, 0::2], s[:, 1::2]], axis=1)
    fh, fl = halves(split_cols)
    table_yf = np.concatenate([fh, fh, fl], axis=1)
    ih, il = halves(split_cols.T)
    table_yi = np.concatenate([ih, ih, il], axis=1)
    block = np.kron(np.eye(2), sine_table(NZ))
    bh, bl = halves(block)
    table_z = np.concatenate([bh, bl], axis=1)
    ly, lz, lx = eigen_values(NY), eigen_values(NZ), eigen_values(NX)
    sum_yz = ly[:, None] + np.tile(lz, 2)[None, :] + screening
    sum_x = np.repeat(lx.reshape(NX // 2, 2), NZ, axis=1)
    return (
        table_x,
        table_yf,
        table_yi,
        table_z,
        sum_yz.astype(np.float32),
        sum_x.astype(np.float32),
    )


def split(v):
    high = v.astype(bf16)
    low = (v - high.astype(f32)).astype(bf16)
    return high, low


def dot(a, b):
    return jnp.dot(a, b, preferred_element_type=f32)


def dot_nt(a, b):
    return lax.dot_general(a, b, (((1,), (1,)), ((), ())), preferred_element_type=f32)


def iota(shape, dim):
    return lax.broadcasted_iota(jnp.int32, shape, dim)


def one_hot(cond):
    return jnp.where(cond, 1.0, 0.0).astype(bf16)


def z_product(v, table_z):
    high, low = split(v)
    a = dot(high, table_z)
    return a[:, :LANES] + a[:, LANES:] + dot(low, table_z[:, :LANES])


def kernel(
    orb_hbm, rotation_hbm, tile_hbm, mask_hbm, tx_hbm, tyf_hbm, tyi_hbm, tz_hbm, syz_hbm, sx_hbm,
    out_ref,
    rotation_ref, tile_ref, mask_ref, tx_ref, tyf_ref, tyi_ref, tz_ref, syz_ref, sx_ref,
    own, got, sel_i, sel_j, sel_t, rot_k, rot_j, green, dens,
    ra, rb, box, mid, pot, ra2, rb2, back, term, gathered,
    in_sem, out_sem, table_sem,
    a1_r, b1_r, x_ra, x_rb, c1_r, d1_r, c2_r, d2_r,
    e1_r, e4_r, e1_s, a1_s, b1_s, a2_s, b2_s, c1_s, d1_s, c2_s, d2_s, e4_s,
):
    o = lax.axis_index("orb")
    g = lax.axis_index("grid")
    x, y = o // YDIM, o % YDIM
    z, c = g // 2, g % 2

    def step_of(i):
        return (YDIM - i) // 2 * (1 - 2 * (i % 2))

    def ahead(j, i):
        return (x + DX[j]) % XDIM * YDIM + (y + YDIM + step_of(i)) % YDIM

    def behind(j, i):
        return (x + XDIM - DX[j]) % XDIM * YDIM + (y + YDIM - step_of(i)) % YDIM

    def block(j):
        return pl.ds(pl.multiple_of((x + DX[j]) % XDIM * YDIM, YDIM), YDIM)

    def chunk(j):
        return pl.ds(j * YDIM, YDIM)

    def z_peer(i):
        return (z + ZDIM + step_of(i)) % ZDIM

    def peers(j):
        return YDIM - 1 if DX[j] == 0 else YDIM

    def to_orb(src, dst, s_sem, r_sem, o2):
        pltpu.make_async_remote_copy(
            src_ref=src, dst_ref=dst, send_sem=s_sem, recv_sem=r_sem,
            device_id=(o2, g), device_id_type=MESH,
        ).start()

    def to_grid(src, dst, s_sem, r_sem, g2):
        pltpu.make_async_remote_copy(
            src_ref=src, dst_ref=dst, send_sem=s_sem, recv_sem=r_sem,
            device_id=(o, g2), device_id_type=MESH,
        ).start()

    def here(src, dst, r_sem):
        pltpu.make_async_copy(src, dst, r_sem).start()

    def arrived(ref, sem):
        pltpu.make_async_copy(ref, ref, sem).wait()

    loads = [
        (orb_hbm.at[n], own.at[pl.ds(2 * n, 2), :], in_sem.at[n]) for n in range(4)
    ]
    fetches = [
        (tile_hbm, tile_ref), (mask_hbm, mask_ref), (rotation_hbm, rotation_ref),
        (syz_hbm, syz_ref), (sx_hbm, sx_ref), (tz_hbm, tz_ref),
        (tx_hbm, tx_ref), (tyf_hbm, tyf_ref), (tyi_hbm, tyi_ref),
    ]
    for args in loads:
        pltpu.make_async_copy(*args).start()
    for n, (src, dst) in enumerate(fetches):
        pltpu.make_async_copy(src, dst, table_sem.at[n]).start()
    barrier = pltpu.get_barrier_semaphore()
    for j in range(XDIM):

        @pl.loop(0, peers(j))
        def _(i):
            pl.semaphore_signal(barrier, inc=1, device_id=(ahead(j, i), g), device_id_type=MESH)

    @pl.loop(0, ZDIM - 1)
    def _(i):
        pl.semaphore_signal(barrier, inc=1, device_id=(o, 2 * z_peer(i)), device_id_type=MESH)
        pl.semaphore_signal(barrier, inc=1, device_id=(o, 2 * z_peer(i) + 1), device_id_type=MESH)

    pl.semaphore_signal(barrier, inc=1, device_id=(o, 2 * z + 1 - c), device_id_type=MESH)
    for args in loads:
        pltpu.make_async_copy(*args).wait()
    pl.semaphore_wait(barrier, N_ORB - 1 + N_GRID - 1)

    def cells(o2):
        return pl.ds(pl.multiple_of(o2 * LANES, LANES), LANES)

    for j in range(XDIM):

        @pl.loop(0, peers(j))
        def _(i):
            o2 = ahead(j, i)
            to_orb(own.at[:, cells(o2)], got.at[o], e1_s, e1_r, o2)

    here(own.at[:, cells(o)], got.at[o], e1_r)

    for n, (src, dst) in enumerate(fetches):
        pltpu.make_async_copy(src, dst, table_sem.at[n]).wait()
    in_tile = one_hot(iota((64, NPAIR), 1) // 16 == iota((64, NPAIR), 0))
    corners = 4.0 * dot(tile_ref[...].astype(f32).astype(bf16), in_tile)
    p_row = iota((1, NPAIR), 1)
    target = corners[0:1, :] + (p_row // 4 % 4).astype(f32)
    source = corners[1:2, :] + (p_row % 4).astype(f32)
    half = (iota((256, NPAIR), 0) // 2).astype(f32)
    hot_i = one_hot(half == target)
    hot_j = one_hot(half == source)
    orb_row = iota((NORB, NPAIR), 0).astype(f32)
    mask_of = dot(mask_ref[...].astype(f32).astype(bf16), one_hot(orb_row == source))
    live = jnp.sum(jnp.where(orb_row == target, mask_of, 0.0), axis=0, keepdims=True)
    before = one_hot(iota((LANES, LANES), 0) < iota((LANES, LANES), 1))
    every = jnp.ones((LANES, LANES), bf16)
    running = jnp.zeros((8, LANES), f32)
    ranks = []
    for n in range(NPAIR // LANES):
        flags = jnp.broadcast_to(live[:, n * LANES : (n + 1) * LANES], (8, LANES))
        bits = flags.astype(bf16)
        rank = dot(bits, before) + running
        running = running + dot(bits, every)
        ranks.append(jnp.where(flags > 0.5, rank, -1.0)[0:1, :])
    rank = jnp.concatenate(ranks, axis=1)

    same_plane = iota((PREP, 256), 0) % 2 == iota((PREP, 256), 1) % 2

    def select_rows(r, carry):
        rows = pl.ds(pl.multiple_of(r * PREP, PREP), PREP)
        slot = ((iota((PREP, NPAIR), 0) + r * PREP) // 2).astype(f32)
        chosen = one_hot(slot == rank)
        sel_i[rows, :] = jnp.where(same_plane, dot_nt(chosen, hot_i), 0.0).astype(bf16)
        sel_j[rows, :] = jnp.where(same_plane, dot_nt(chosen, hot_j), 0.0).astype(bf16)
        sel_t[r] = jnp.where(same_plane, dot_nt(hot_i, chosen), 0.0).astype(bf16)
        return carry

    lax.fori_loop(0, ROWS // PREP, select_rows, 0)

    widen = one_hot(iota((256, NORB), 0) // 2 == iota((256, NORB), 1))
    widen_t = one_hot(iota((NORB, 256), 0) == iota((NORB, 256), 1) // 2)
    for n, part in enumerate(split(rotation_ref[...])):
        tall = dot_nt(widen, part).astype(bf16)
        rot_k[n] = jnp.where(same_plane, dot(tall, widen_t), 0.0).astype(bf16)

    def fill_green(n, carry):
        green[n] = coupling / (syz_ref[...] + sx_ref[pl.ds(n, 1), :])
        return carry

    lax.fori_loop(0, NX // 2, fill_green, 0)

    arrived(got, e1_r)

    got_h, got_l = split(got[...].reshape(256, LANES))
    rotated = dot(rot_k[0], got_h) + dot(rot_k[0], got_l) + dot(rot_k[1], got_h)
    rotated = jnp.concatenate(split(rotated), axis=1)

    def density_rows(r, carry):
        rows = pl.ds(pl.multiple_of(r * 128, 128), 128)
        wide_i = dot(sel_i[rows, :], rotated)
        wide_j = dot(sel_j[rows, :], rotated)
        at_j = wide_j[:, :LANES] + wide_j[:, LANES:]
        rot_j[rows, :] = at_j
        density = (wide_i[:, :LANES] + wide_i[:, LANES:]) * at_j
        spectrum = z_product(density, tz_ref[...])
        dens[pl.ds(r * 4, 4)] = spectrum.reshape(4, 32, LANES)
        return carry

    lax.fori_loop(0, ROWS // 128, density_rows, 0)

    ours = pl.ds(2 * g, 2)

    def z_rows(z2):
        return pl.ds(2 * z2, 2)

    def z_rows_b(z2):
        return pl.ds(16 + 2 * z2, 2)

    for j in range(XDIM):

        @pl.loop(0, peers(j))
        def _(i):
            o2 = ahead(j, i)
            to_orb(dens.at[o2, pl.ds(0, 16), :], ra.at[j * YDIM + i], a1_s, a1_r.at[j], o2)

        @pl.loop(0, ZDIM - 1)
        def _(i):
            z2 = z_peer(i)
            to_grid(
                dens.at[block(j), z_rows_b(z2), :], rb.at[block(j), ours, :], b1_s, b1_r.at[j], 2 * z2 + 1
            )

        @pl.when(c == 1)
        def _():
            here(dens.at[block(j), z_rows_b(z), :], rb.at[block(j), ours, :], b1_r.at[j])

        @pl.when(c == 0)
        def _():
            to_grid(
                dens.at[block(j), z_rows_b(z), :], rb.at[block(j), ours, :], b1_s, b1_r.at[j], 2 * z + 1
            )

    here(dens.at[o, pl.ds(0, 16), :], ra.at[N_ORB - 1], a1_r.at[XDIM - 1])

    for j in range(XDIM):
        arrived(ra.at[chunk(j)], a1_r.at[j])

        @pl.loop(0, ZDIM - 1)
        def _(i):
            z2 = z_peer(i)
            to_grid(ra.at[chunk(j), z_rows(z2), :], box.at[chunk(j), ours, :], a2_s, x_ra.at[j], 2 * z2)

        @pl.when(c == 0)
        def _():
            here(ra.at[chunk(j), z_rows(z), :], box.at[chunk(j), ours, :], x_ra.at[j])

        @pl.when(c == 1)
        def _():
            to_grid(ra.at[chunk(j), z_rows(z), :], box.at[chunk(j), ours, :], a2_s, x_ra.at[j], 2 * z)
            arrived(rb.at[block(j)], b1_r.at[j])

            @pl.loop(0, peers(j))
            def _(i):
                o2 = ahead(j, i)
                to_orb(rb.at[o2], box.at[j * YDIM + i], b2_s, x_rb.at[j], o2)

            if DX[j] == 0:
                here(rb.at[o], box.at[N_ORB - 1], x_rb.at[j])

    for j in range(XDIM):

        @pl.when(c == 0)
        def _():
            arrived(box.at[chunk(j)], x_ra.at[j])

        @pl.when(c == 1)
        def _():
            arrived(box.at[chunk(j)], x_rb.at[j])

        for h in range(2):
            places = [j * YDIM + h * 4 + n for n in range(4)]
            v = jnp.concatenate([box[p] for p in places], axis=1)
            high, low = split(v)
            w = dot(tx_ref[...], jnp.concatenate([high, low, high], axis=0))
            for n in range(4):
                start = pl.multiple_of(behind(j, h * 4 + n) * NX, NX)
                mid[pl.ds(start, NX), :] = w[:, n * LANES : (n + 1) * LANES]

    low_half = iota((N_ORB, LANES), 1) < NZ

    for n in range(NX // 2):
        v0 = mid[pl.ds(2 * n, N_ORB, stride=NX), :]
        v1 = mid[pl.ds(2 * n + 1, N_ORB, stride=NX), :]
        even = jnp.where(low_half, v0, pltpu.roll(v1, NZ, 1))
        odd = jnp.where(low_half, pltpu.roll(v0, NZ, 1), v1)
        high, low = split(jnp.concatenate([even, odd], axis=0))
        spectrum = dot(tyf_ref[...], jnp.concatenate([high, low, high], axis=0)) * green[n]
        high, low = split(spectrum)
        w = dot(tyi_ref[...], jnp.concatenate([high, low, high], axis=0))
        even, odd = w[:N_ORB], w[N_ORB:]
        mid[pl.ds(2 * n, N_ORB, stride=NX), :] = jnp.where(low_half, even, pltpu.roll(odd, NZ, 1))
        mid[pl.ds(2 * n + 1, N_ORB, stride=NX), :] = jnp.where(low_half, pltpu.roll(even, NZ, 1), odd)

    for j in range(XDIM):
        for h in range(2):
            starts = [pl.multiple_of(behind(j, h * 4 + n) * NX, NX) for n in range(4)]
            v = jnp.concatenate([mid[pl.ds(s, NX), :] for s in starts], axis=1)
            high, low = split(v)
            w = dot(tx_ref[...], jnp.concatenate([high, low, high], axis=0))
            for n in range(4):
                pot[j * YDIM + h * 4 + n] = w[:, n * LANES : (n + 1) * LANES]

        @pl.when(c == 0)
        def _():
            @pl.loop(0, 2 * (ZDIM - 1))
            def _(i):
                g2 = 2 * z_peer(i // 2) + i % 2
                to_grid(
                    pot.at[chunk(j), pl.ds(2 * g2, 2), :], ra2.at[chunk(j), z_rows(z), :],
                    c1_s, c1_r.at[j], g2,
                )

            to_grid(
                pot.at[chunk(j), pl.ds(2 * (2 * z + 1), 2), :], ra2.at[chunk(j), z_rows(z), :],
                c1_s, c1_r.at[j], 2 * z + 1,
            )
            here(pot.at[chunk(j), ours, :], ra2.at[chunk(j), z_rows(z), :], c1_r.at[j])

        @pl.when(c == 1)
        def _():
            @pl.loop(0, peers(j))
            def _(i):
                to_orb(pot.at[j * YDIM + i], rb2.at[o], d1_s, d1_r.at[j], behind(j, i))

            if DX[j] == 0:
                here(pot.at[N_ORB - 1], rb2.at[o], d1_r.at[j])

    for j in range(XDIM):
        arrived(ra2.at[chunk(j)], c1_r.at[j])

        @pl.loop(0, peers(j))
        def _(i):
            to_orb(
                ra2.at[j * YDIM + i], back.at[o, pl.ds(0, 16), :], c2_s, c2_r.at[j], behind(j, i)
            )

        if DX[j] == 0:
            here(ra2.at[N_ORB - 1], back.at[o, pl.ds(0, 16), :], c2_r.at[j])

        @pl.when(c == 1)
        def _():
            arrived(rb2.at[block(j)], d1_r.at[j])

            @pl.loop(0, 2 * (ZDIM - 1))
            def _(i):
                g2 = 2 * z_peer(i // 2) + i % 2
                to_grid(
                    rb2.at[block(j), pl.ds(2 * g2, 2), :], back.at[block(j), z_rows_b(z), :],
                    d2_s, d2_r.at[j], g2,
                )

            to_grid(
                rb2.at[block(j), pl.ds(2 * (2 * z), 2), :], back.at[block(j), z_rows_b(z), :],
                d2_s, d2_r.at[j], 2 * z,
            )
            here(rb2.at[block(j), ours, :], back.at[block(j), z_rows_b(z), :], d2_r.at[j])

    total = jnp.zeros((256, 2 * LANES), f32)
    for j in range(XDIM):
        r = (x + DX[j]) % XDIM
        arrived(back.at[block(j), pl.ds(0, 16), :], c2_r.at[j])
        arrived(back.at[block(j), pl.ds(16, 16), :], d2_r.at[j])
        rows = pl.ds(pl.multiple_of(r * PREP, PREP), PREP)
        potential = z_product(back[block(j)].reshape(PREP, LANES), tz_ref[...])
        products = jnp.concatenate(split(potential * rot_j[rows, :]), axis=1)
        total = total + dot(sel_t[r], products)
    term[...] = (-(total[:, :LANES] + total[:, LANES:])).reshape(N_ORB, 8, LANES)

    for j in range(XDIM):

        @pl.loop(0, peers(j))
        def _(i):
            o2 = ahead(j, i)
            to_orb(term.at[o2], gathered.at[:, cells(o)], e4_s, e4_r, o2)

    here(term.at[o], gathered.at[:, cells(o)], e4_r)

    most = pl.ds(0, N_ORB - 1)
    arrived(got.at[most], e1_s)
    arrived(ra.at[most], a1_s)
    arrived(term.at[most], e4_s)
    arrived(ra2.at[most], c2_s)

    @pl.when(c == 0)
    def _():
        arrived(rb.at[:, pl.ds(0, 16), :], b1_s)
        arrived(ra.at[:, pl.ds(0, 14), :], a2_s)
        arrived(pot.at[:, pl.ds(0, 30), :], c1_s)

    @pl.when(c == 1)
    def _():
        arrived(rb.at[:, pl.ds(0, 14), :], b1_s)
        arrived(ra.at[:, pl.ds(0, 16), :], a2_s)
        arrived(rb.at[most], b2_s)
        arrived(pot.at[most], d1_s)
        arrived(rb2.at[:, pl.ds(0, 30), :], d2_s)

    arrived(gathered, e4_r)
    stores = [
        (gathered.at[pl.ds(2 * n, 2), :], out_ref.at[n], out_sem.at[n]) for n in range(4)
    ]
    for args in stores:
        pltpu.make_async_copy(*args).start()
    for args in stores:
        pltpu.make_async_copy(*args).wait()


def on_device(orbitals, rotation, tile_list, pair_mask):
    consts = [jnp.asarray(t) for t in tables()]
    anyspace = pl.BlockSpec(memory_space=pl.ANY)
    dma = pltpu.SemaphoreType.DMA
    box = pltpu.VMEM((N_ORB, NX, LANES), f32)
    half_box = pltpu.VMEM((N_ORB, 16, LANES), f32)
    operands = [rotation, tile_list.T, pair_mask, *consts]
    return pl.pallas_call(
        kernel,
        out_shape=jax.ShapeDtypeStruct(orbitals.shape, f32),
        in_specs=[anyspace] * (4 + len(consts)),
        out_specs=anyspace,
        scratch_shapes=[pltpu.VMEM(a.shape, a.dtype) for a in operands]
        + [
            pltpu.VMEM((8, NY * NZ), f32),
            pltpu.VMEM((N_ORB, 8, LANES), f32),
            pltpu.VMEM((ROWS, 256), bf16),
            pltpu.VMEM((ROWS, 256), bf16),
            pltpu.VMEM((ROWS // PREP, 256, PREP), bf16),
            pltpu.VMEM((2, 256, 256), bf16),
            pltpu.VMEM((ROWS, LANES), f32),
            pltpu.VMEM((NX // 2, NY, LANES), f32),
            box,
            half_box,
            box,
            box,
            pltpu.VMEM((N_ORB * NX, LANES), f32),
            box,
            half_box,
            box,
            box,
            pltpu.VMEM((N_ORB, 8, LANES), f32),
            pltpu.VMEM((8, NY * NZ), f32),
            dma((4,)),
            dma((4,)),
            dma((len(operands),)),
        ]
        + [dma((XDIM,))] * 8
        + [dma] * 12,
        compiler_params=pltpu.CompilerParams(
            collective_id=0, has_side_effects=True, vmem_limit_bytes=67_000_000
        ),
    )(orbitals, *operands)


def solution(mesh):
    in_specs = (P("orb", "grid", None), P(), P(), P())
    out_specs = P("orb", "grid", None)
    return jax.shard_map(
        on_device, mesh=mesh, in_specs=in_specs, out_specs=out_specs, check_vma=False
    )
```

time: 81 us -> 66.4 us (0.82)
  Pallas kernels: 73.3 us -> 64.7 us
  local copies, waits for them, and re-layouts: 7.07 us -> 1.57 us
    pallas_call x1, Pallas kernels: 73.3 us -> 64.7 us  [on_device(): pl.pallas_call(kernel, out_shape=jax.ShapeDtypeStruct(orbitals.shape, f32...]
    unnamed x20 -> x1, local copies, waits for them, and re-layouts: 7.07 us -> 1.57 us
where the time goes in v2:
time: 66.4 us; the launch traced here: 66.3 us
  Pallas kernels  64.7 us (97%)
  local copies, waits for them, and re-layouts  1.57 us (2%)
    pallas_call x1, Pallas kernels, on_device(): pl.pallas_call(kernel, out_shape=jax.ShapeDtypeStruct(orbitals.shape, f32...  64.7 us
    unnamed x1, local copies, waits for them, and re-layouts  1.57 us

profile of v2, /device:TPU:1, one launch (start us, length us, event | category | flops | bytes accessed | tf_op | source)
XLA Modules:
  0.0 66.3 jit_solution(5945856488471729462)
XLA Ops:
  0.0 64.7 %shard_map.100 = f32[4,2,4096]{2,1,0:T(2,128)} custom-call(f32[4,2,4096]{2,1,0:T(2,128)} %orb_hbm.1, f32[128,128]{1,0:T(8,128)} %rotation_hbm.1, s32[2,64]{1,0:T(2,128)} %bitcast.1, s32[128,128]{1,0:T(8,128)} %mask_hbm.1, bf16[32,96]{1,0:T(8,128)(2,1)} %constant.12.clone.tx_hbm, bf16[64,192]{1,0:T(8,128)(2,1)} %constant.13.clone.tyf_hbm, ...), custom_call_target="tpu_custom_call" | custom-call | tf_op jit(solution)/shard_map/pallas_call | solution.py:477
  64.8 1.6 %copy.12 = f32[4,2,4096]{2,1,0:T(2,128)} copy(f32[4,2,4096]{2,1,0:T(2,128)} %shard_map.100) | data formatting | bytes 262144

commit v3 on v2

--- a/solution.py
+++ b/solution.py
@@ -17,7 +17,13 @@
 XDIM = 4
 YDIM = 8
 ZDIM = 8
-DX = (2, 1, 3, 0)
+CHUNKS = 4
+CHUNK = 8
+PEERS = sorted(
+    ((dx, dy) for dx in (2, 1, -1, 0) for dy in (4, 3, -3, 2, -2, 1, -1, 0)),
+    key=lambda step: -abs(step[0]) - abs(step[1]),
+)
+Z_STEPS = (4, 3, -3, 2, -2, 1, -1)
 ROWS = 1024
 PREP = 256
 coupling = 0.25
@@ -111,26 +117,22 @@
     x, y = o // YDIM, o % YDIM
     z, c = g // 2, g % 2
 
-    def step_of(i):
-        return (YDIM - i) // 2 * (1 - 2 * (i % 2))
-
-    def ahead(j, i):
-        return (x + DX[j]) % XDIM * YDIM + (y + YDIM + step_of(i)) % YDIM
-
-    def behind(j, i):
-        return (x + XDIM - DX[j]) % XDIM * YDIM + (y + YDIM - step_of(i)) % YDIM
-
-    def block(j):
-        return pl.ds(pl.multiple_of((x + DX[j]) % XDIM * YDIM, YDIM), YDIM)
+    def ahead(k):
+        dx, dy = PEERS[k]
+        return (x + dx % XDIM) % XDIM * YDIM + (y + dy % YDIM) % YDIM
+
+    def behind(k):
+        dx, dy = PEERS[k]
+        return (x + -dx % XDIM) % XDIM * YDIM + (y + -dy % YDIM) % YDIM
 
     def chunk(j):
-        return pl.ds(j * YDIM, YDIM)
-
-    def z_peer(i):
-        return (z + ZDIM + step_of(i)) % ZDIM
-
-    def peers(j):
-        return YDIM - 1 if DX[j] == 0 else YDIM
+        return pl.ds(j * CHUNK, CHUNK)
+
+    def members(j):
+        return range(j * CHUNK, min((j + 1) * CHUNK, N_ORB - 1))
+
+    others = range(N_ORB - 1)
+    z_peers = [(z + step % ZDIM) % ZDIM for step in Z_STEPS]
 
     def to_orb(src, dst, s_sem, r_sem, o2):
         pltpu.make_async_remote_copy(
@@ -163,17 +165,11 @@
     for n, (src, dst) in enumerate(fetches):
         pltpu.make_async_copy(src, dst, table_sem.at[n]).start()
     barrier = pltpu.get_barrier_semaphore()
-    for j in range(XDIM):
-
-        @pl.loop(0, peers(j))
-        def _(i):
-            pl.semaphore_signal(barrier, inc=1, device_id=(ahead(j, i), g), device_id_type=MESH)
-
-    @pl.loop(0, ZDIM - 1)
-    def _(i):
-        pl.semaphore_signal(barrier, inc=1, device_id=(o, 2 * z_peer(i)), device_id_type=MESH)
-        pl.semaphore_signal(barrier, inc=1, device_id=(o, 2 * z_peer(i) + 1), device_id_type=MESH)
-
+    for k in others:
+        pl.semaphore_signal(barrier, inc=1, device_id=(ahead(k), g), device_id_type=MESH)
+    for z2 in z_peers:
+        for core in range(2):
+            pl.semaphore_signal(barrier, inc=1, device_id=(o, 2 * z2 + core), device_id_type=MESH)
     pl.semaphore_signal(barrier, inc=1, device_id=(o, 2 * z + 1 - c), device_id_type=MESH)
     for args in loads:
         pltpu.make_async_copy(*args).wait()
@@ -182,13 +178,8 @@
     def cells(o2):
         return pl.ds(pl.multiple_of(o2 * LANES, LANES), LANES)
 
-    for j in range(XDIM):
-
-        @pl.loop(0, peers(j))
-        def _(i):
-            o2 = ahead(j, i)
-            to_orb(own.at[:, cells(o2)], got.at[o], e1_s, e1_r, o2)
-
+    for k in others:
+        to_orb(own.at[:, cells(ahead(k))], got.at[o], e1_s, e1_r, ahead(k))
     here(own.at[:, cells(o)], got.at[o], e1_r)
 
     for n, (src, dst) in enumerate(fetches):
@@ -218,16 +209,17 @@
 
     same_plane = iota((PREP, 256), 0) % 2 == iota((PREP, 256), 1) % 2
 
-    def select_rows(r, carry):
-        rows = pl.ds(pl.multiple_of(r * PREP, PREP), PREP)
-        slot = ((iota((PREP, NPAIR), 0) + r * PREP) // 2).astype(f32)
-        chosen = one_hot(slot == rank)
+    slot = (iota((32, NPAIR), 0) // 2).astype(f32)
+    for j in range(CHUNKS):
+        rows = pl.ds(j * PREP, PREP)
+        parts = [
+            one_hot(slot == rank - (16 * ahead(k)).astype(f32))
+            for k in range(j * CHUNK, (j + 1) * CHUNK)
+        ]
+        chosen = jnp.concatenate(parts, axis=0)
         sel_i[rows, :] = jnp.where(same_plane, dot_nt(chosen, hot_i), 0.0).astype(bf16)
         sel_j[rows, :] = jnp.where(same_plane, dot_nt(chosen, hot_j), 0.0).astype(bf16)
-        sel_t[r] = jnp.where(same_plane, dot_nt(hot_i, chosen), 0.0).astype(bf16)
-        return carry
-
-    lax.fori_loop(0, ROWS // PREP, select_rows, 0)
+        sel_t[j] = jnp.where(same_plane, dot_nt(hot_i, chosen), 0.0).astype(bf16)
 
     widen = one_hot(iota((256, NORB), 0) // 2 == iota((256, NORB), 1))
     widen_t = one_hot(iota((NORB, 256), 0) == iota((NORB, 256), 1) // 2)
@@ -247,18 +239,16 @@
     rotated = dot(rot_k[0], got_h) + dot(rot_k[0], got_l) + dot(rot_k[1], got_h)
     rotated = jnp.concatenate(split(rotated), axis=1)
 
-    def density_rows(r, carry):
-        rows = pl.ds(pl.multiple_of(r * 128, 128), 128)
-        wide_i = dot(sel_i[rows, :], rotated)
-        wide_j = dot(sel_j[rows, :], rotated)
-        at_j = wide_j[:, :LANES] + wide_j[:, LANES:]
-        rot_j[rows, :] = at_j
-        density = (wide_i[:, :LANES] + wide_i[:, LANES:]) * at_j
-        spectrum = z_product(density, tz_ref[...])
-        dens[pl.ds(r * 4, 4)] = spectrum.reshape(4, 32, LANES)
-        return carry
-
-    lax.fori_loop(0, ROWS // 128, density_rows, 0)
+    def density_rows(j):
+        for h in range(2):
+            rows = pl.ds(j * PREP + h * 128, 128)
+            wide_i = dot(sel_i[rows, :], rotated)
+            wide_j = dot(sel_j[rows, :], rotated)
+            at_j = wide_j[:, :LANES] + wide_j[:, LANES:]
+            rot_j[rows, :] = at_j
+            density = (wide_i[:, :LANES] + wide_i[:, LANES:]) * at_j
+            spectrum = z_product(density, tz_ref[...])
+            dens[pl.ds(j * CHUNK + h * 4, 4)] = spectrum.reshape(4, 32, LANES)
 
     ours = pl.ds(2 * g, 2)
 
@@ -268,38 +258,31 @@
     def z_rows_b(z2):
         return pl.ds(16 + 2 * z2, 2)
 
-    for j in range(XDIM):
-
-        @pl.loop(0, peers(j))
-        def _(i):
-            o2 = ahead(j, i)
-            to_orb(dens.at[o2, pl.ds(0, 16), :], ra.at[j * YDIM + i], a1_s, a1_r.at[j], o2)
-
-        @pl.loop(0, ZDIM - 1)
-        def _(i):
-            z2 = z_peer(i)
+    last = N_ORB - 1
+    for j in range(CHUNKS):
+        density_rows(j)
+        for k in members(j):
+            to_orb(dens.at[k, pl.ds(0, 16), :], ra.at[k], a1_s, a1_r.at[j], ahead(k))
+        for z2 in z_peers:
             to_grid(
-                dens.at[block(j), z_rows_b(z2), :], rb.at[block(j), ours, :], b1_s, b1_r.at[j], 2 * z2 + 1
+                dens.at[chunk(j), z_rows_b(z2), :], rb.at[chunk(j), ours, :], b1_s, b1_r.at[j], 2 * z2 + 1
             )
 
         @pl.when(c == 1)
         def _():
-            here(dens.at[block(j), z_rows_b(z), :], rb.at[block(j), ours, :], b1_r.at[j])
+            here(dens.at[chunk(j), z_rows_b(z), :], rb.at[chunk(j), ours, :], b1_r.at[j])
 
         @pl.when(c == 0)
         def _():
             to_grid(
-                dens.at[block(j), z_rows_b(z), :], rb.at[block(j), ours, :], b1_s, b1_r.at[j], 2 * z + 1
+                dens.at[chunk(j), z_rows_b(z), :], rb.at[chunk(j), ours, :], b1_s, b1_r.at[j], 2 * z + 1
             )
 
-    here(dens.at[o, pl.ds(0, 16), :], ra.at[N_ORB - 1], a1_r.at[XDIM - 1])
-
-    for j in range(XDIM):
+    here(dens.at[last, pl.ds(0, 16), :], ra.at[last], a1_r.at[CHUNKS - 1])
+
+    for j in range(CHUNKS):
         arrived(ra.at[chunk(j)], a1_r.at[j])
-
-        @pl.loop(0, ZDIM - 1)
-        def _(i):
-            z2 = z_peer(i)
+        for z2 in z_peers:
             to_grid(ra.at[chunk(j), z_rows(z2), :], box.at[chunk(j), ours, :], a2_s, x_ra.at[j], 2 * z2)
 
         @pl.when(c == 0)
@@ -309,17 +292,13 @@
         @pl.when(c == 1)
         def _():
             to_grid(ra.at[chunk(j), z_rows(z), :], box.at[chunk(j), ours, :], a2_s, x_ra.at[j], 2 * z)
-            arrived(rb.at[block(j)], b1_r.at[j])
-
-            @pl.loop(0, peers(j))
-            def _(i):
-                o2 = ahead(j, i)
-                to_orb(rb.at[o2], box.at[j * YDIM + i], b2_s, x_rb.at[j], o2)
-
-            if DX[j] == 0:
-                here(rb.at[o], box.at[N_ORB - 1], x_rb.at[j])
-
-    for j in range(XDIM):
+            arrived(rb.at[chunk(j)], b1_r.at[j])
+            for k in members(j):
+                to_orb(rb.at[k], box.at[k], b2_s, x_rb.at[j], ahead(k))
+            if j == CHUNKS - 1:
+                here(rb.at[last], box.at[last], x_rb.at[j])
+
+    for j in range(CHUNKS):
 
         @pl.when(c == 0)
         def _():
@@ -330,12 +309,12 @@
             arrived(box.at[chunk(j)], x_rb.at[j])
 
         for h in range(2):
-            places = [j * YDIM + h * 4 + n for n in range(4)]
-            v = jnp.concatenate([box[p] for p in places], axis=1)
+            places = [j * CHUNK + h * 4 + n for n in range(4)]
+            v = jnp.concatenate([box[k] for k in places], axis=1)
             high, low = split(v)
             w = dot(tx_ref[...], jnp.concatenate([high, low, high], axis=0))
-            for n in range(4):
-                start = pl.multiple_of(behind(j, h * 4 + n) * NX, NX)
+            for n, k in enumerate(places):
+                start = pl.multiple_of(behind(k) * NX, NX)
                 mid[pl.ds(start, NX), :] = w[:, n * LANES : (n + 1) * LANES]
 
     low_half = iota((N_ORB, LANES), 1) < NZ
@@ -353,25 +332,26 @@
         mid[pl.ds(2 * n, N_ORB, stride=NX), :] = jnp.where(low_half, even, pltpu.roll(odd, NZ, 1))
         mid[pl.ds(2 * n + 1, N_ORB, stride=NX), :] = jnp.where(low_half, pltpu.roll(even, NZ, 1), odd)
 
-    for j in range(XDIM):
+    for j in range(CHUNKS):
         for h in range(2):
-            starts = [pl.multiple_of(behind(j, h * 4 + n) * NX, NX) for n in range(4)]
-            v = jnp.concatenate([mid[pl.ds(s, NX), :] for s in starts], axis=1)
+            places = [j * CHUNK + h * 4 + n for n in range(4)]
+            v = jnp.concatenate(
+                [mid[pl.ds(pl.multiple_of(behind(k) * NX, NX), NX), :] for k in places], axis=1
+            )
             high, low = split(v)
             w = dot(tx_ref[...], jnp.concatenate([high, low, high], axis=0))
-            for n in range(4):
-                pot[j * YDIM + h * 4 + n] = w[:, n * LANES : (n + 1) * LANES]
+            for n, k in enumerate(places):
+                pot[k] = w[:, n * LANES : (n + 1) * LANES]
 
         @pl.when(c == 0)
         def _():
-            @pl.loop(0, 2 * (ZDIM - 1))
-            def _(i):
-                g2 = 2 * z_peer(i // 2) + i % 2
-                to_grid(
-                    pot.at[chunk(j), pl.ds(2 * g2, 2), :], ra2.at[chunk(j), z_rows(z), :],
-                    c1_s, c1_r.at[j], g2,
-                )
-
+            for z2 in z_peers:
+                for core in range(2):
+                    g2 = 2 * z2 + core
+                    to_grid(
+                        pot.at[chunk(j), pl.ds(2 * g2, 2), :], ra2.at[chunk(j), z_rows(z), :],
+                        c1_s, c1_r.at[j], g2,
+                    )
             to_grid(
                 pot.at[chunk(j), pl.ds(2 * (2 * z + 1), 2), :], ra2.at[chunk(j), z_rows(z), :],
                 c1_s, c1_r.at[j], 2 * z + 1,
@@ -380,61 +360,46 @@
 
         @pl.when(c == 1)
         def _():
-            @pl.loop(0, peers(j))
-            def _(i):
-                to_orb(pot.at[j * YDIM + i], rb2.at[o], d1_s, d1_r.at[j], behind(j, i))
-
-            if DX[j] == 0:
-                here(pot.at[N_ORB - 1], rb2.at[o], d1_r.at[j])
-
-    for j in range(XDIM):
+            for k in members(j):
+                to_orb(pot.at[k], rb2.at[k], d1_s, d1_r.at[j], behind(k))
+            if j == CHUNKS - 1:
+                here(pot.at[last], rb2.at[last], d1_r.at[j])
+
+    for j in range(CHUNKS):
         arrived(ra2.at[chunk(j)], c1_r.at[j])
-
-        @pl.loop(0, peers(j))
-        def _(i):
-            to_orb(
-                ra2.at[j * YDIM + i], back.at[o, pl.ds(0, 16), :], c2_s, c2_r.at[j], behind(j, i)
-            )
-
-        if DX[j] == 0:
-            here(ra2.at[N_ORB - 1], back.at[o, pl.ds(0, 16), :], c2_r.at[j])
+        for k in members(j):
+            to_orb(ra2.at[k], back.at[k, pl.ds(0, 16), :], c2_s, c2_r.at[j], behind(k))
+        if j == CHUNKS - 1:
+            here(ra2.at[last], back.at[last, pl.ds(0, 16), :], c2_r.at[j])
 
         @pl.when(c == 1)
         def _():
-            arrived(rb2.at[block(j)], d1_r.at[j])
-
-            @pl.loop(0, 2 * (ZDIM - 1))
-            def _(i):
-                g2 = 2 * z_peer(i // 2) + i % 2
-                to_grid(
-                    rb2.at[block(j), pl.ds(2 * g2, 2), :], back.at[block(j), z_rows_b(z), :],
-                    d2_s, d2_r.at[j], g2,
-                )
-
+            arrived(rb2.at[chunk(j)], d1_r.at[j])
+            for z2 in z_peers:
+                for core in range(2):
+                    g2 = 2 * z2 + core
+                    to_grid(
+                        rb2.at[chunk(j), pl.ds(2 * g2, 2), :], back.at[chunk(j), z_rows_b(z), :],
+                        d2_s, d2_r.at[j], g2,
+                    )
             to_grid(
-                rb2.at[block(j), pl.ds(2 * (2 * z), 2), :], back.at[block(j), z_rows_b(z), :],
+                rb2.at[chunk(j), pl.ds(2 * (2 * z), 2), :], back.at[chunk(j), z_rows_b(z), :],
                 d2_s, d2_r.at[j], 2 * z,
             )
-            here(rb2.at[block(j), ours, :], back.at[block(j), z_rows_b(z), :], d2_r.at[j])
+            here(rb2.at[chunk(j), ours, :], back.at[chunk(j), z_rows_b(z), :], d2_r.at[j])
 
     total = jnp.zeros((256, 2 * LANES), f32)
-    for j in range(XDIM):
-        r = (x + DX[j]) % XDIM
-        arrived(back.at[block(j), pl.ds(0, 16), :], c2_r.at[j])
-        arrived(back.at[block(j), pl.ds(16, 16), :], d2_r.at[j])
-        rows = pl.ds(pl.multiple_of(r * PREP, PREP), PREP)
-        potential = z_product(back[block(j)].reshape(PREP, LANES), tz_ref[...])
+    for j in range(CHUNKS):
+        arrived(back.at[chunk(j), pl.ds(0, 16), :], c2_r.at[j])
+        arrived(back.at[chunk(j), pl.ds(16, 16), :], d2_r.at[j])
+        rows = pl.ds(j * PREP, PREP)
+        potential = z_product(back[chunk(j)].reshape(PREP, LANES), tz_ref[...])
         products = jnp.concatenate(split(potential * rot_j[rows, :]), axis=1)
-        total = total + dot(sel_t[r], products)
+        total = total + dot(sel_t[j], products)
     term[...] = (-(total[:, :LANES] + total[:, LANES:])).reshape(N_ORB, 8, LANES)
 
-    for j in range(XDIM):
-
-        @pl.loop(0, peers(j))
-        def _(i):
-            o2 = ahead(j, i)
-            to_orb(term.at[o2], gathered.at[:, cells(o)], e4_s, e4_r, o2)
-
+    for k in others:
+        to_orb(term.at[ahead(k)], gathered.at[:, cells(o)], e4_s, e4_r, ahead(k))
     here(term.at[o], gathered.at[:, cells(o)], e4_r)
 
     most = pl.ds(0, N_ORB - 1)
@@ -504,7 +469,7 @@
             dma((4,)),
             dma((len(operands),)),
         ]
-        + [dma((XDIM,))] * 8
+        + [dma((CHUNKS,))] * 8
         + [dma] * 12,
         compiler_params=pltpu.CompilerParams(
             collective_id=0, has_side_effects=True, vmem_limit_bytes=67_000_000

time: 66.4 us -> 63.3 us (0.953)
  Pallas kernels: 64.7 us -> 61.6 us
    pallas_call x1, Pallas kernels: 64.7 us -> 61.6 us  [on_device(): pl.pallas_call(kernel, out_shape=jax.ShapeDtypeStruct(orbitals.shape, f32...]
where the time goes in v3:
time: 63.3 us; the launch traced here: 63.1 us
  Pallas kernels  61.6 us (97%)
  local copies, waits for them, and re-layouts  1.57 us (2%)
    pallas_call x1, Pallas kernels, on_device(): pl.pallas_call(kernel, out_shape=jax.ShapeDtypeStruct(orbitals.shape, f32...  61.6 us
    unnamed x1, local copies, waits for them, and re-layouts  1.57 us

profile of v3, /device:TPU:1, one launch (start us, length us, event | category | flops | bytes accessed | tf_op | source)
XLA Modules:
  0.0 63.1 jit_solution(11113118513909931341)
XLA Ops:
  0.0 61.6 %shard_map.100 = f32[4,2,4096]{2,1,0:T(2,128)} custom-call(f32[4,2,4096]{2,1,0:T(2,128)} %orb_hbm.1, f32[128,128]{1,0:T(8,128)} %rotation_hbm.1, s32[2,64]{1,0:T(2,128)} %bitcast.1, s32[128,128]{1,0:T(8,128)} %mask_hbm.1, bf16[32,96]{1,0:T(8,128)(2,1)} %constant.12.clone.tx_hbm, bf16[64,192]{1,0:T(8,128)(2,1)} %constant.13.clone.tyf_hbm, ...), custom_call_target="tpu_custom_call" | custom-call | tf_op jit(solution)/shard_map/pallas_call | solution.py:442
  61.6 1.6 %copy.12 = f32[4,2,4096]{2,1,0:T(2,128)} copy(f32[4,2,4096]{2,1,0:T(2,128)} %shard_map.100) | data formatting | bytes 262144

commit v4 on v3

--- a/solution.py
+++ b/solution.py
@@ -160,10 +160,6 @@
         (syz_hbm, syz_ref), (sx_hbm, sx_ref), (tz_hbm, tz_ref),
         (tx_hbm, tx_ref), (tyf_hbm, tyf_ref), (tyi_hbm, tyi_ref),
     ]
-    for args in loads:
-        pltpu.make_async_copy(*args).start()
-    for n, (src, dst) in enumerate(fetches):
-        pltpu.make_async_copy(src, dst, table_sem.at[n]).start()
     barrier = pltpu.get_barrier_semaphore()
     for k in others:
         pl.semaphore_signal(barrier, inc=1, device_id=(ahead(k), g), device_id_type=MESH)
@@ -171,6 +167,10 @@
         for core in range(2):
             pl.semaphore_signal(barrier, inc=1, device_id=(o, 2 * z2 + core), device_id_type=MESH)
     pl.semaphore_signal(barrier, inc=1, device_id=(o, 2 * z + 1 - c), device_id_type=MESH)
+    for args in loads:
+        pltpu.make_async_copy(*args).start()
+    for n, (src, dst) in enumerate(fetches):
+        pltpu.make_async_copy(src, dst, table_sem.at[n]).start()
     for args in loads:
         pltpu.make_async_copy(*args).wait()
     pl.semaphore_wait(barrier, N_ORB - 1 + N_GRID - 1)
@@ -239,16 +239,15 @@
     rotated = dot(rot_k[0], got_h) + dot(rot_k[0], got_l) + dot(rot_k[1], got_h)
     rotated = jnp.concatenate(split(rotated), axis=1)
 
-    def density_rows(j):
-        for h in range(2):
-            rows = pl.ds(j * PREP + h * 128, 128)
-            wide_i = dot(sel_i[rows, :], rotated)
-            wide_j = dot(sel_j[rows, :], rotated)
-            at_j = wide_j[:, :LANES] + wide_j[:, LANES:]
-            rot_j[rows, :] = at_j
-            density = (wide_i[:, :LANES] + wide_i[:, LANES:]) * at_j
-            spectrum = z_product(density, tz_ref[...])
-            dens[pl.ds(j * CHUNK + h * 4, 4)] = spectrum.reshape(4, 32, LANES)
+    def density_rows(j, h):
+        rows = pl.ds(j * PREP + h * 128, 128)
+        wide_i = dot(sel_i[rows, :], rotated)
+        wide_j = dot(sel_j[rows, :], rotated)
+        at_j = wide_j[:, :LANES] + wide_j[:, LANES:]
+        rot_j[rows, :] = at_j
+        density = (wide_i[:, :LANES] + wide_i[:, LANES:]) * at_j
+        spectrum = z_product(density, tz_ref[...])
+        dens[pl.ds(j * CHUNK + h * 4, 4)] = spectrum.reshape(4, 32, LANES)
 
     ours = pl.ds(2 * g, 2)
 
@@ -260,9 +259,10 @@
 
     last = N_ORB - 1
     for j in range(CHUNKS):
-        density_rows(j)
-        for k in members(j):
-            to_orb(dens.at[k, pl.ds(0, 16), :], ra.at[k], a1_s, a1_r.at[j], ahead(k))
+        for h in range(2):
+            density_rows(j, h)
+            for k in members(j)[h * 4 : h * 4 + 4]:
+                to_orb(dens.at[k, pl.ds(0, 16), :], ra.at[k], a1_s, a1_r.at[j], ahead(k))
         for z2 in z_peers:
             to_grid(
                 dens.at[chunk(j), z_rows_b(z2), :], rb.at[chunk(j), ours, :], b1_s, b1_r.at[j], 2 * z2 + 1
@@ -319,18 +319,26 @@
 
     low_half = iota((N_ORB, LANES), 1) < NZ
 
-    for n in range(NX // 2):
-        v0 = mid[pl.ds(2 * n, N_ORB, stride=NX), :]
-        v1 = mid[pl.ds(2 * n + 1, N_ORB, stride=NX), :]
-        even = jnp.where(low_half, v0, pltpu.roll(v1, NZ, 1))
-        odd = jnp.where(low_half, pltpu.roll(v0, NZ, 1), v1)
-        high, low = split(jnp.concatenate([even, odd], axis=0))
-        spectrum = dot(tyf_ref[...], jnp.concatenate([high, low, high], axis=0)) * green[n]
+    def plane(kx):
+        return pl.ds(kx, N_ORB, stride=NX)
+
+    for n in range(NX // 4):
+        evens, odds = [], []
+        for kx in (4 * n, 4 * n + 2):
+            v0, v1 = mid[plane(kx), :], mid[plane(kx + 1), :]
+            evens.append(jnp.where(low_half, v0, pltpu.roll(v1, NZ, 1)))
+            odds.append(jnp.where(low_half, pltpu.roll(v0, NZ, 1), v1))
+        v = jnp.concatenate([jnp.concatenate(evens, axis=1), jnp.concatenate(odds, axis=1)], axis=0)
+        high, low = split(v)
+        spectrum = dot(tyf_ref[...], jnp.concatenate([high, low, high], axis=0))
+        spectrum = spectrum * jnp.concatenate([green[2 * n], green[2 * n + 1]], axis=1)
         high, low = split(spectrum)
         w = dot(tyi_ref[...], jnp.concatenate([high, low, high], axis=0))
-        even, odd = w[:N_ORB], w[N_ORB:]
-        mid[pl.ds(2 * n, N_ORB, stride=NX), :] = jnp.where(low_half, even, pltpu.roll(odd, NZ, 1))
-        mid[pl.ds(2 * n + 1, N_ORB, stride=NX), :] = jnp.where(low_half, pltpu.roll(even, NZ, 1), odd)
+        for h, kx in enumerate((4 * n, 4 * n + 2)):
+            part = w[:, h * LANES : (h + 1) * LANES]
+            even, odd = part[:N_ORB], part[N_ORB:]
+            mid[plane(kx), :] = jnp.where(low_half, even, pltpu.roll(odd, NZ, 1))
+            mid[plane(kx + 1), :] = jnp.where(low_half, pltpu.roll(even, NZ, 1), odd)
 
     for j in range(CHUNKS):
         for h in range(2):

time: 63.3 us -> 62.3 us (0.984)
  Pallas kernels: 61.6 us -> 60.6 us
    pallas_call x1, Pallas kernels: 61.6 us -> 60.6 us  [on_device(): pl.pallas_call(kernel, out_shape=jax.ShapeDtypeStruct(orbitals.shape, f32...]
where the time goes in v4:
time: 62.3 us; the launch traced here: 62.1 us
  Pallas kernels  60.6 us (97%)
  local copies, waits for them, and re-layouts  1.57 us (3%)
    pallas_call x1, Pallas kernels, on_device(): pl.pallas_call(kernel, out_shape=jax.ShapeDtypeStruct(orbitals.shape, f32...  60.6 us
    unnamed x1, local copies, waits for them, and re-layouts  1.57 us

profile of v4, /device:TPU:1, one launch (start us, length us, event | category | flops | bytes accessed | tf_op | source)
XLA Modules:
  0.0 62.1 jit_solution(7899672833048613119)
XLA Ops:
  0.0 60.6 %shard_map.100 = f32[4,2,4096]{2,1,0:T(2,128)} custom-call(f32[4,2,4096]{2,1,0:T(2,128)} %orb_hbm.1, f32[128,128]{1,0:T(8,128)} %rotation_hbm.1, s32[2,64]{1,0:T(2,128)} %bitcast.1, s32[128,128]{1,0:T(8,128)} %mask_hbm.1, bf16[32,96]{1,0:T(8,128)(2,1)} %constant.12.clone.tx_hbm, bf16[64,192]{1,0:T(8,128)(2,1)} %constant.13.clone.tyf_hbm, ...), custom_call_target="tpu_custom_call" | custom-call | tf_op jit(solution)/shard_map/pallas_call | solution.py:450
  60.6 1.6 %copy.12 = f32[4,2,4096]{2,1,0:T(2,128)} copy(f32[4,2,4096]{2,1,0:T(2,128)} %shard_map.100) | data formatting | bytes 262144

commit v5 on v4

--- a/solution.py
+++ b/solution.py
@@ -236,7 +236,8 @@
     arrived(got, e1_r)
 
     got_h, got_l = split(got[...].reshape(256, LANES))
-    rotated = dot(rot_k[0], got_h) + dot(rot_k[0], got_l) + dot(rot_k[1], got_h)
+    wide = dot(rot_k[0], jnp.concatenate([got_h, got_l], axis=1))
+    rotated = wide[:, :LANES] + wide[:, LANES:] + dot(rot_k[1], got_h)
     rotated = jnp.concatenate(split(rotated), axis=1)
 
     def density_rows(j, h):
@@ -374,12 +375,6 @@
                 here(pot.at[last], rb2.at[last], d1_r.at[j])
 
     for j in range(CHUNKS):
-        arrived(ra2.at[chunk(j)], c1_r.at[j])
-        for k in members(j):
-            to_orb(ra2.at[k], back.at[k, pl.ds(0, 16), :], c2_s, c2_r.at[j], behind(k))
-        if j == CHUNKS - 1:
-            here(ra2.at[last], back.at[last, pl.ds(0, 16), :], c2_r.at[j])
-
         @pl.when(c == 1)
         def _():
             arrived(rb2.at[chunk(j)], d1_r.at[j])
@@ -395,6 +390,12 @@
                 d2_s, d2_r.at[j], 2 * z,
             )
             here(rb2.at[chunk(j), ours, :], back.at[chunk(j), z_rows_b(z), :], d2_r.at[j])
+
+        arrived(ra2.at[chunk(j)], c1_r.at[j])
+        for k in members(j):
+            to_orb(ra2.at[k], back.at[k, pl.ds(0, 16), :], c2_s, c2_r.at[j], behind(k))
+        if j == CHUNKS - 1:
+            here(ra2.at[last], back.at[last, pl.ds(0, 16), :], c2_r.at[j])
 
     total = jnp.zeros((256, 2 * LANES), f32)
     for j in range(CHUNKS):

time: 62.3 us -> 62.8 us (level)
  no operation moved by 1% of the time
where the time goes in v5:
time: 62.8 us; the launch traced here: 62.6 us
  Pallas kernels  61 us (97%)
  local copies, waits for them, and re-layouts  1.57 us (2%)
    pallas_call x1, Pallas kernels, on_device(): pl.pallas_call(kernel, out_shape=jax.ShapeDtypeStruct(orbitals.shape, f32...  61 us
    unnamed x1, local copies, waits for them, and re-layouts  1.57 us

profile of v5, /device:TPU:1, one launch (start us, length us, event | category | flops | bytes accessed | tf_op | source)
XLA Modules:
  0.0 62.6 jit_solution(3834096847132615175)
XLA Ops:
  0.0 61.0 %shard_map.100 = f32[4,2,4096]{2,1,0:T(2,128)} custom-call(f32[4,2,4096]{2,1,0:T(2,128)} %orb_hbm.1, f32[128,128]{1,0:T(8,128)} %rotation_hbm.1, s32[2,64]{1,0:T(2,128)} %bitcast.1, s32[128,128]{1,0:T(8,128)} %mask_hbm.1, bf16[32,96]{1,0:T(8,128)(2,1)} %constant.12.clone.tx_hbm, bf16[64,192]{1,0:T(8,128)(2,1)} %constant.13.clone.tyf_hbm, ...), custom_call_target="tpu_custom_call" | custom-call | tf_op jit(solution)/shard_map/pallas_call | solution.py:451
  61.0 1.6 %copy.12 = f32[4,2,4096]{2,1,0:T(2,128)} copy(f32[4,2,4096]{2,1,0:T(2,128)} %shard_map.100) | data formatting | bytes 262144
